TPU v7x, 512 devices: a 4x2x32 block of a 4x8x32 slice. The times are simulated.
512 devices in a mesh: member: 2 (over y), seq: 32 (over z), head: 4 (over x), rep: 2 (over core).
Axes of the slice: x: 4, y: 2, z: 32, core: 2. Of those that a mesh axis runs over, the one named last changes fastest.
The devices are a block of a 4x8x32 slice.
Arguments:
- x_raw: bfloat16 [4, 32768, 2560], P(('member', 'rep'), 'seq', 'head'), parts along dimension 0, may hold values from -6 to 6
- bc_raw: bfloat16 [4, 32768, 256], P(('member', 'rep'), 'seq'), parts along dimension 0, may hold values from -3 to 3
- gate_in: bfloat16 [4, 32768, 2560], P(('member', 'rep'), 'seq', 'head'), parts along dimension 0, may hold values from -570 to 570
- step_raw: float32 [4, 32768, 40], P(('member', 'rep'), 'seq', 'head'), parts along dimension 0, may hold values from -1.9 to 4.9
- conv_x_weight: bfloat16 [8, 2560], P('member', 'head'), parts along dimension 0, may hold values from -3 to 3
- conv_x_bias: bfloat16 [5120], P(('member', 'head')), parts along dimension 0, may hold values from -0.5 to 0.5
- conv_bc_weight: bfloat16 [8, 256], P('member'), parts along dimension 0, may hold values from -3 to 3
- conv_bc_bias: bfloat16 [512], P('member'), parts along dimension 0, may hold values from -0.5 to 0.5
- dt_bias: float32 [80], P(('member', 'head')), parts along dimension 0, may hold values from -3.5 to 0.55
- a_log: float32 [80], P(('member', 'head')), parts along dimension 0
- d_skip: float32 [80], P(('member', 'head')), parts along dimension 0, may hold values from 0.5 to 2
- norm_gain: float32 [5120], P(('member', 'head')), parts along dimension 0, may hold values from 0.5 to 1.5
Outputs:
- mixer_out: bfloat16 [4, 32768, 2560], P(('member', 'rep'), 'seq', 'head'), parts along dimension 0
There are 2 independent parts, one for each index of `member`. A program takes and returns all parts, laid end to end along the dimension named above; each array names one. Nothing has to cross between parts.
All inputs are finite; a program needn't handle non-finite values.
Results may differ from a plain program's by a relative error of at most 0.0082.
Values may be sent and summed in bfloat16 or wider, within the bound.
A program may use at most 64 MiB of HBM per device.

v0:
```python
import jax
import jax.numpy as jnp
from jax import lax
from jax.sharding import PartitionSpec as P

HEADDIM = 64
STATE = 128
GROUP = 256
CONV = 4
DI = 2560


norm_eps = 1e-05


def carried_in_2(value, axis, join, neutral):
    count, mine = (lax.axis_size(axis), lax.axis_index(axis))
    pieces = jax.tree.map(lambda part: lax.all_gather(part, axis), value)
    so_far = jax.tree.map(
        lambda part, zero: jnp.full_like(part, 0) + jnp.asarray(zero, part.dtype), value, neutral
    )

    def step(position, so_far):
        longer = join(so_far, jax.tree.map(lambda part: part[position], pieces))
        return jax.tree.map(lambda new, old: jnp.where(position < mine, new, old), longer, so_far)

    return lax.fori_loop(0, count - 1, step, so_far)


def passed_along(value, axis, by):
    size = lax.axis_size(axis)
    pairs = [(i, i + by) for i in range(size) if 0 <= i + by < size]
    return lax.ppermute(value, axis, pairs)


def shard_conv(extended, conv_weight, conv_bias, row_count):
    summed = jnp.zeros(
        (extended.shape[0], row_count, extended.shape[2]), jnp.float32
    ) + conv_bias.astype(jnp.float32)
    for tap_index in range(CONV):
        summed = summed + conv_weight[tap_index].astype(jnp.float32) * extended[
            :, tap_index : tap_index + row_count
        ].astype(jnp.float32)
    return jax.nn.silu(summed).astype(jnp.bfloat16)


def entry_boundary(device_decay, device_state, zero_state):

    def join_states(earlier, later):
        return (earlier[0] * later[0], earlier[1] * later[0][:, None, None] + later[1])

    prefix = carried_in_2(
        (device_decay, device_state), "seq", join_states, (jnp.ones_like(device_decay), zero_state)
    )
    return prefix[1]


def on_device(
    x_raw,
    bc_raw,
    gate_in,
    step_raw,
    conv_x_weight,
    conv_x_bias,
    conv_bc_weight,
    conv_bc_bias,
    dt_bias,
    a_log,
    d_skip,
    norm_gain,
):
    local_len = x_raw.shape[1]
    feat_local = x_raw.shape[2]
    heads_local = dt_bias.shape[0]
    rim_rows = jnp.concatenate(
        (x_raw[:, local_len - CONV + 1 :, :], bc_raw[:, local_len - CONV + 1 :, :]), axis=2
    )
    before = passed_along(rim_rows, "seq", 1)
    x_conv = shard_conv(
        jnp.concatenate((before[:, :, :feat_local], x_raw), axis=1),
        conv_x_weight,
        conv_x_bias,
        local_len,
    )
    bc_conv = shard_conv(
        jnp.concatenate((before[:, :, feat_local:], bc_raw), axis=1),
        conv_bc_weight,
        conv_bc_bias,
        local_len,
    )
    step_size = jax.nn.softplus(step_raw[0] + dt_bias)
    log_rate = -jnp.exp(a_log) * step_size
    groups = local_len // GROUP
    x_heads = x_conv[0].reshape(groups, GROUP, heads_local, HEADDIM)
    b_rows = bc_conv[0, :, :STATE].reshape(groups, GROUP, STATE)
    c_rows = bc_conv[0, :, STATE:].reshape(groups, GROUP, STATE)
    step_groups = step_size.reshape(groups, GROUP, heads_local)
    log_decay = jnp.cumsum(log_rate.reshape(groups, GROUP, heads_local), axis=1)
    group_decay = jnp.exp(log_decay[:, -1, :])
    tail_weight = jnp.exp(log_decay[:, -1:, :] - log_decay) * step_groups
    weighted = (tail_weight[..., None] * x_heads.astype(jnp.float32)).astype(jnp.bfloat16)
    fresh_state = jnp.einsum("cshp,csn->chpn", weighted, b_rows, preferred_element_type=jnp.float32)

    def advance(carried_in, group_terms):
        state_now, decay_now = carried_in
        decay_group, fresh_group = group_terms
        return (
            (decay_group[:, None, None] * state_now + fresh_group, decay_now * decay_group),
            (state_now, decay_now),
        )

    zero_state = jnp.zeros((heads_local, HEADDIM, STATE), jnp.float32)
    (device_state, device_decay), (entry_local, entry_decay) = lax.scan(
        advance, (zero_state, jnp.ones((heads_local,), jnp.float32)), (group_decay, fresh_state)
    )
    intersection = jnp.einsum("ctn,csn->cts", c_rows, b_rows, preferred_element_type=jnp.float32)
    lower_mask = jnp.arange(GROUP)[:, None] >= jnp.arange(GROUP)[None, :]
    head_decay = jnp.swapaxes(log_decay, 1, 2)
    spread = head_decay[:, :, :, None] - head_decay[:, :, None, :]
    kernel = jnp.where(lower_mask, jnp.exp(jnp.where(lower_mask, spread, 0.0)), 0.0)
    mixing = (
        intersection[:, None] * kernel * jnp.swapaxes(step_groups, 1, 2)[:, :, None, :]
    ).astype(jnp.bfloat16)
    intra_out = jnp.einsum("chts,cshp->cthp", mixing, x_heads, preferred_element_type=jnp.float32)
    c_wide = c_rows.astype(jnp.float32)
    local_part = jnp.einsum("ctn,chpn->cthp", c_wide, entry_local, precision=lax.Precision.HIGHEST)
    incoming = entry_boundary(device_decay, device_state, zero_state)
    correction = jnp.einsum("ctn,hpn->cthp", c_wide, incoming, precision=lax.Precision.HIGHEST)
    carried = local_part + entry_decay[:, None, :, None] * correction
    outputs = intra_out + jnp.exp(log_decay)[..., None] * carried
    mixed_rows = outputs.reshape(local_len, heads_local, HEADDIM) + d_skip[None, :, None] * x_conv[
        0
    ].reshape(local_len, heads_local, HEADDIM).astype(jnp.float32)
    gated_rows = mixed_rows.reshape(local_len, feat_local) * jax.nn.silu(
        gate_in[0].astype(jnp.float32)
    )
    squares = lax.psum(jnp.sum(gated_rows * gated_rows, axis=1, keepdims=True), "head")
    mean_square = squares / DI
    result = (gated_rows * lax.rsqrt(mean_square + norm_eps) * norm_gain).astype(jnp.bfloat16)
    return result[None]


def solution(mesh):
    in_specs = (
        P(("member", "rep"), "seq", "head"),
        P(("member", "rep"), "seq", None),
        P(("member", "rep"), "seq", "head"),
        P(("member", "rep"), "seq", "head"),
        P("member", "head"),
        P(("member", "head")),
        P("member", None),
        P("member"),
        P(("member", "head")),
        P(("member", "head")),
        P(("member", "head")),
        P(("member", "head")),
    )
    out_specs = P(("member", "rep"), "seq", "head")
    return jax.shard_map(
        on_device, mesh=mesh, in_specs=in_specs, out_specs=out_specs, check_vma=False
    )
```

profile of v0, /device:TPU:40, one launch (start us, length us, event | category | flops | bytes accessed | tf_op | source)
XLA Modules:
  0.0 300.2 jit_solution(18378659386302962243)
XLA Ops:
  8.9 4.7 %collective-permute-start = (bf16[1,3,896]{1,2,0:T(8,128)(2,1)}, bf16[1,3,896]{1,2,0:T(8,128)(2,1)S(1)}, u32[]{:S(2)}, u32[]{:S(2)}) collective-permute-start(bf16[1,3,896]{1,2,0:T(8,128)(2,1)} %copy.45), channel_id=1, source_target_pairs={{0,8},{8,16},{16,24},{24,32},{32,40},{40,48},{48,56},{56,64},{64,7... | collective-permute-start | bytes 16136 | tf_op jit(solution)/shard_map/ppermute | solution.py:33
  13.7 0.9 reduce.5
  16.1 2.3 reduce-window.6
  19.6 1.4 fusion.30
  21.9 0.9 convert_reduce_fusion.3
  24.1 2.9 multiply_convert_fusion.3
  27.0 1.9 reshape_squeeze.10
  29.8 1.9 fusion.18
  31.6 13.6 %while.31 = (s32[]{:T(128)}, f32[10,64,128]{2,1,0:T(8,128)S(1)}, f32[10]{0:T(128)}, f32[4,10,64,128]{3,2,1,0:T(8,128)}, f32[4,10]{1,0:T(4,128)}, /*index=5*/f32[...) while((s32[]{:T(128)}, f32[10,64,128]{2,1,0:T(8,128)S(1)}, f32[10]{0:T(128)}, ...), condition=%wide.region_3.4_spmd.clone, body=%wide.region_2.3_spmd.clone.sunk | while | flops 327703 | bytes 1639349 | solution.py:113
  31.7 1.3 fusion.43
  33.8 1.3 dynamic_update_slice.14
  35.1 1.3 fusion.43
  37.2 1.3 dynamic_update_slice.14
  38.5 1.3 fusion.43
  40.6 1.3 dynamic_update_slice.14
  41.9 1.3 fusion.43
  44.0 1.3 dynamic_update_slice.14
  46.7 1.4 copy.55
  48.8 1.6 copy.63
  50.4 2.3 reshape.188
  53.4 1.3 dynamic-slice
  55.7 93.7 %all-reduce = f32[320]{0:T(512)} all-reduce(f32[320]{0:T(512)S(1)} %dynamic-update-slice), channel_id=2, replica_groups=mesh['member'=2,'seq'=32,'head'=4,'rep'=2] {'seq'}, use_global_device_ids=true, to_apply=%add | all-reduce | flops 320 | bytes 2560
  150.1 1.3 fusion.33
  151.4 4.0 %fusion.34 = f32[4,256,10,64]{1,3,2,0:T(8,128)} fusion(bf16[4,256,128,1]{2,1,3,0:T(8,128)(2,1)S(1)} %bitcast.80, f32[4,10,64,128]{3,2,1,0:T(8,128)} %get-tuple-element.139), kind=kOutput, calls=%fused_computation.71 | convolution fusion | flops 1006632960 | bytes 4194304 | tf_op jit(solution)/shard_map/ctn,chpn->cthp/dot_general | solution.py:126
  155.4 70.4 %all-gather.4.cloned.1.call-done = f32[320,64,128]{2,1,0:T(8,128)} async-done(((f32[10,64,128]{2,1,0:T(8,128)}), f32[320,64,128]{2,1,0:T(8,128)}) %all-gather.4.cloned.1.call-update) | async-done | bytes 10485776 | tf_op jit(solution)/shard_map/all_gather | solution.py:18
  225.7 34.8 %while.32 = (s32[]{:T(128)}, f32[10,64,128]{2,1,0:T(8,128)S(1)}, s32[]{:T(128)}, f32[32,10]{1,0:T(8,128)S(1)}, f32[32,10,64,128]{3,2,1,0:T(8,128)}, /*index=5*/s32[]{:T(128)}, s32[]{:T(128)}) while((s32[]{:T(128)}, f32[10,64,128]{2,1,0:T(8,128)S(1)}, s32[]{:T(128)}, f32[32,10]{1,0:T(8,128)S(1)}, f32[32,10,64,128]{3,2,1,0:T(8,128)}, ...), condition=%wide.region_5.6_spmd.clone, body=%wide.region_4.5_spmd.clone.sunk | while | flops 327684 | bytes 983265 | solution.py:27
  225.7 1.1 fusion.44
  226.9 1.1 fusion.44
  228.0 1.1 fusion.44
  229.1 1.1 fusion.44
  230.2 1.1 fusion.44
  231.4 1.1 fusion.44
  232.5 1.1 fusion.44
  233.6 1.1 fusion.44
  234.7 1.1 fusion.44
  235.8 1.1 fusion.44
  237.0 1.1 fusion.44
  238.1 1.1 fusion.44
  239.2 1.1 fusion.44
  240.3 1.1 fusion.44
  241.5 1.1 fusion.44
  242.6 1.1 fusion.44
  243.7 1.1 fusion.44
  244.8 1.1 fusion.44
  246.0 1.1 fusion.44
  247.1 1.1 fusion.44
  248.2 1.1 fusion.44
  249.3 1.1 fusion.44
  250.4 1.1 fusion.44
  251.6 1.1 fusion.44
  252.7 1.1 fusion.44
  253.8 1.1 fusion.44
  254.9 1.1 fusion.44
  256.1 1.1 fusion.44
  257.2 1.1 fusion.44
  258.3 1.1 fusion.44
  259.4 1.1 fusion.44
  260.6 1.2 fusion.25
  262.3 6.9 %fusion.15 = (f32[4,256]{1,0:T(4,128)S(1)}, f32[4,256,10,64]{1,3,2,0:T(8,128)S(1)}) fusion(f32[4,256,10,64]{1,0,3,2:T(4,128)S(1)} %copy-done.1, f32[10]{0:T(128)S(1)} %copy-done.12, bf16[4,256,10,64]{1,0,3,2:T(4,128)(2,1)} %reshape_squeeze.10, f32[4,256,10,64]{1,3,2,0:T(8,128)} %fusion.34, f32[4,256,10,64]{1,3,2,0:T(8,128)S(1)} %fusion.25, ...), kind=kOutput, calls=%fused_computation.24 | convolution fusion | flops 360446976 | bytes 13037768 | tf_op jit(solution)/shard_map/chts,cshp->cthp/dot_general | solution.py:124
  269.2 3.2 %copy.62 = f32[4,256,10,64]{1,0,3,2:T(4,128)} copy(f32[4,256,10,64]{1,3,2,0:T(8,128)S(1)} %get-tuple-element.227) | data formatting | bytes 5242880 | tf_op jit(solution)/shard_map/add | solution.py:130
  272.4 4.3 %reshape.179 = f32[1,1024,640]{1,2,0:T(8,128)} reshape(f32[4,256,10,64]{1,0,3,2:T(4,128)} %copy.62) | data formatting | bytes 5242880 | tf_op jit(solution)/shard_map/reshape | solution.py:131
  276.7 10.2 %psum.7 = f32[1024,1]{0,1:T(1,128)S(1)} all-reduce(f32[1024,1]{0,1:T(1,128)S(1)} %bitcast.87), channel_id=1, replica_groups=mesh['member'=2,'seq'=32,'head'=4,'rep'=2] {'head'}, use_global_device_ids=true, to_apply=%region_7.8 | all-reduce | flops 1024 | bytes 8192 | tf_op jit(solution)/shard_map/psum | solution.py:137
  287.0 3.9 %multiply_convert_fusion.2 = bf16[1,1024,640]{1,2,0:T(8,128)(2,1)} fusion(f32[1,1024,640]{1,2,0:T(8,128)} %reshape.179, bf16[1,1024,640]{1,2,0:T(8,128)(2,1)S(1)} %multiply_convert_fusion.3, f32[640]{0:T(1024)S(1)} %copy-done.9, f32[1024]{0:T(1024)S(1)} %bitcast.88, f32[640]{0:T(1024)S(1)} %copy-done.7, bf16[1,1024,640]{1,2,0:T(8,128)(2,1)S(1)} %copy.63), kind=kLoop, calls=%fused_computation.26 | loop fusion | flops 7864320 | bytes 6562816 | tf_op jit(solution)/shard_map/convert_element_type | solution.py:139
  291.0 2.4 copy.66
  (118 shorter events, 16.2 us)
Async XLA Ops:
  6.5 16.2 %copy-start.2 = (bf16[1,1024,640]{2,1,0:T(8,128)(2,1)S(1)}, bf16[1,1024,640]{2,1,0:T(8,128)(2,1)}, u32[]{:S(2)}) copy-start(bf16[1,1024,640]{2,1,0:T(8,128)(2,1)} %param.16) | copy-start | bytes 3932164
  6.5 17.5 %copy-start.10 = (bf16[640]{0:T(1024)(128)(2,1)S(1)}, bf16[640]{0:T(1024)(128)(2,1)}, u32[]{:S(2)}) copy-start(bf16[640]{0:T(1024)(128)(2,1)} %param.21) | copy-start | bytes 3844
  6.6 17.5 %copy-start.14 = (bf16[256]{0:T(256)(128)(2,1)S(1)}, bf16[256]{0:T(256)(128)(2,1)}, u32[]{:S(2)}) copy-start(bf16[256]{0:T(256)(128)(2,1)} %param.23) | copy-start | bytes 1540
  6.6 219.2 %all-gather.4.cloned.1.call-start = ((), (), s32[]{:S(2)}) async-start(), calls=%async_computation | async-start | bytes 10813440 | tf_op jit(solution)/shard_map/all_gather | solution.py:18
  8.9 15.1 %collective-permute-start = (bf16[1,3,896]{1,2,0:T(8,128)(2,1)}, bf16[1,3,896]{1,2,0:T(8,128)(2,1)S(1)}, u32[]{:S(2)}, u32[]{:S(2)}) collective-permute-start(bf16[1,3,896]{1,2,0:T(8,128)(2,1)} %copy.45), channel_id=1, source_target_pairs={{0,8},{8,16},{16,24},{24,32},{32,40},{40,48},{48,56},{56,64},{64,7... | collective-permute-start | bytes 16136 | tf_op jit(solution)/shard_map/ppermute | solution.py:33
  27.0 2.0 copy-start.3
  45.3 0.7 copy-start
  50.4 2.3 copy-start.11
  50.4 5.0 %copy-start.8 = (f32[10]{0:T(128)S(1)}, f32[10]{0:T(128)}, u32[]{:S(2)}) copy-start(f32[10]{0:T(128)} %get-tuple-element.141) | copy-start | bytes 124
  260.5 1.7 copy-start.1
  260.5 1.7 copy-start.4
  260.5 1.7 copy-start.5
  260.6 1.7 copy-start.6
  260.6 1.7 copy-start.12
  260.6 1.7 copy-start.13
  272.4 14.6 %copy-start.7 = (f32[640]{0:T(1024)S(1)}, f32[640]{0:T(1024)}, u32[]{:S(2)}) copy-start(f32[640]{0:T(1024)} %mul.251) | copy-start | bytes 7684
  272.4 14.6 %copy-start.9 = (f32[640]{0:T(1024)S(1)}, f32[640]{0:T(1024)}, u32[]{:S(2)}) copy-start(f32[640]{0:T(1024)} %param.27) | copy-start | bytes 7684
Sparse Core Ops, SparseCore 0:
  46.2 179.4 all-gather.3
where the time goes:
time: 302 us; the launch traced here: 300 us
  blocking collectives  104 us (34%)
  waiting for transfers between devices  70.4 us (23%)
  other arithmetic  57.4 us (19%)
  local copies, waits for them, and re-layouts  33.2 us (11%)
  matrix products  15.2 us (5%)
  between operations  14.4 us (5%)
  starting transfers between devices  4.71 us (2%)
    unnamed x1, blocking collectives  93.7 us
    all_gather x1, waiting for transfers between devices, carried_in_2(): pieces = jax.tree.map(lambda part: lax.all_gather(part, axis), value)  70.4 us
    select_n x31, other arithmetic, step(): jnp.where(position < mine, new, old)  33.5 us
    psum x1, blocking collectives, on_device(): lax.psum(jnp.sum(gated_rows * gated_rows, axis=1, keepdims=True), 'head')  10.2 us
    dot_general x1, matrix products, on_device(): jnp.einsum('chts,cshp->cthp', mixing, x_heads, preferred_element_type=jnp...  6.92 us
  transfers between devices with their start and end apart: 2, of which 1 were waited for; matrix products, arithmetic and copies ran while one was open for 8% of the time, Pallas kernels for 0%

commit v1 on v0

v1 whole, which is shorter than its diff:
```python
import functools

import jax
import jax.numpy as jnp
from jax import lax
from jax.experimental import pallas as pl
from jax.experimental.pallas import tpu as pltpu
from jax.sharding import PartitionSpec as P

HEADDIM = 64
STATE = 128
GROUP = 256
CONV = 4
LANES = 128
HALO = 16
ROWS = 64
SEG = 8
LOG2E = 1.4426950408889634
norm_eps = 1e-05

F32 = jnp.float32
BF16 = jnp.bfloat16
MESH = pl.DeviceIdType.MESH


def silu(v):
    half = 0.5 * v
    return half + half * jnp.tanh(half)


def two_parts(v):
    high = v.astype(BF16)
    return high, (v - high.astype(F32)).astype(BF16)


def three_parts(v):
    high = v.astype(BF16)
    rest = v - high.astype(F32)
    mid = rest.astype(BF16)
    return high, mid, (rest - mid.astype(F32)).astype(BF16)


def dot(a, b, dims=((1,), (0,))):
    return lax.dot_general(a, b, (dims, ((), ())), preferred_element_type=F32)


def kernel(sizes, *refs):
    n_seq, n_head, seg_len, length, feat, heads = sizes
    (
        x_hbm, bc_hbm, gate_hbm, step_ref, cxw_ref, cxb_ref, cbw_ref, cbb_ref,
        dt_ref, alog_ref, skip_ref, gain_ref, out_ref,
        xext, bcext, gbuf, xconv, bconv, stepb, ldb, ldt, stept, par, cw, expand_m, tri_m,
        tail_e, weighted, fresh, entry, base, scale, dec,
        s_send, a_recv, ld_mine, ld_recv, loc, t_send, b_recv, lt_mine, lt_recv, c_send, inc,
        ss_mine, ss_recv,
        loc_sem, halo_s, halo_r, a_s, a_r, al_s, al_r, b_s, b_r, bl_s, bl_r, c_s, c_r, x_s, x_r,
    ) = refs
    groups = length // GROUP
    tiles = feat // LANES
    piece = STATE // seg_len
    segs = n_seq // seg_len
    di = feat * n_head

    me = lax.axis_index("seq")
    mine_h = lax.axis_index("head")
    seg = me // seg_len
    pos = lax.rem(me, seg_len)

    loads = [
        pltpu.make_async_copy(x_hbm, xext.at[pl.ds(HALO, length)], loc_sem.at[0]),
        pltpu.make_async_copy(bc_hbm, bcext.at[pl.ds(HALO, length)], loc_sem.at[1]),
        pltpu.make_async_copy(gate_hbm, gbuf, loc_sem.at[2]),
    ]
    for load in loads:
        load.start()

    b_recv[...] = jnp.zeros_like(b_recv)
    lt_recv[...] = jnp.zeros_like(lt_recv)
    barrier = pltpu.get_barrier_semaphore()
    following = lax.rem(me + 1, n_seq)
    partners = [{"seq": following}, {"seq": lax.rem(me + n_seq - 1, n_seq)}]
    for d in range(1, seg_len):
        partners.append({"seq": seg * seg_len + lax.rem(pos + d, seg_len)})
    for k in range(1, segs):
        partners.append({"seq": lax.rem(me + k * seg_len, n_seq)})
    for d in range(1, n_head):
        partners.append({"head": lax.rem(mine_h + d, n_head)})
    for partner in partners:
        pl.semaphore_signal(barrier, inc=1, device_id=partner, device_id_type=MESH)

    row_i = lax.broadcasted_iota(jnp.int32, (GROUP, GROUP), 0)
    col_i = lax.broadcasted_iota(jnp.int32, (GROUP, GROUP), 1)
    tri_m[...] = jnp.where(row_i >= col_i, 1.0, 0.0).astype(BF16)
    head_i = lax.broadcasted_iota(jnp.int32, (LANES, feat), 0)
    feat_i = lax.broadcasted_iota(jnp.int32, (LANES, feat), 1)
    expand_m[...] = jnp.where((feat_i >> 6) == head_i, 1.0, 0.0).astype(BF16)
    par[...] = jnp.zeros_like(par)
    par[0:1, 0:heads] = dt_ref[...]
    par[1:2, 0:heads] = alog_ref[...]
    par[2:3, 0:heads] = skip_ref[...]
    cw[0:CONV, 0:feat] = cxw_ref[...].astype(F32)
    cw[CONV : CONV + 1, 0:feat] = cxb_ref[...].astype(F32)
    cw[0:CONV, feat:] = cbw_ref[...].astype(F32)
    cw[CONV : CONV + 1, feat:] = cbb_ref[...].astype(F32)

    def widen3(v):
        total = None
        for part in three_parts(v):
            term = dot(part, expand_m[...])
            total = term if total is None else total + term
        return total

    def widen2(v):
        high, low = two_parts(v)
        return dot(high, expand_m[...]) + dot(low, expand_m[...])

    stepb[...] = jnp.zeros_like(stepb)
    stepb[:, 0:heads] = step_ref[...]
    rate = -LOG2E * jnp.exp(par[1:2, :])

    def decays(g, carry):
        r0 = pl.multiple_of(g * GROUP, GROUP)
        raw = stepb[pl.ds(r0, GROUP), :] + par[0:1, :]
        step = jnp.maximum(raw, 0.0) + jnp.log1p(jnp.exp(-jnp.abs(raw)))
        stepb[pl.ds(r0, GROUP), :] = step
        total = None
        for part in three_parts(rate * step):
            term = dot(tri_m[...], part)
            total = term if total is None else total + term
        ldb[pl.ds(r0, GROUP), :] = total
        dec[pl.ds(g, 1), :] = total[GROUP - 1 : GROUP, :]
        return carry

    dec[...] = jnp.zeros_like(dec)
    lax.fori_loop(0, groups, decays, 0)
    ld_total = dec[0:1, :]
    for g in range(1, groups):
        ld_total = ld_total + dec[g : g + 1, :]
    ld_mine[...] = ld_total[None]

    def conv(ext, r, c0, width, tile, w_off):
        block = ext[pl.ds(r, ROWS + HALO), c0 : c0 + width].astype(F32)
        lo = w_off + c0
        acc = cw[CONV : CONV + 1, lo : lo + width]
        for k in range(CONV):
            shift = CONV - 1 - k
            moved = block if shift == 0 else pltpu.roll(block, shift, 0)
            acc = acc + cw[k : k + 1, lo : lo + width] * moved[HALO:]
        return silu(acc)

    def states(g, carry):
        r0 = pl.multiple_of(g * GROUP, GROUP)
        ld = ldb[pl.ds(r0, GROUP), :]
        tail = jnp.exp2(ld[GROUP - 1 : GROUP, :] - ld) * stepb[pl.ds(r0, GROUP), :]
        tail_e[...] = widen2(tail)

        def chunk(i, inner):
            q0 = pl.multiple_of(i * ROWS, ROWS)
            r = pl.multiple_of(r0 + q0, ROWS)
            for j in range(2 * STATE // LANES):
                bconv[pl.ds(r, ROWS), j * LANES : (j + 1) * LANES] = conv(
                    bcext, r, j * LANES, LANES, j, feat
                ).astype(BF16)
            for j in range(tiles):
                c0 = j * LANES
                value = conv(xext, r, c0, LANES, j, 0).astype(BF16)
                xconv[pl.ds(r, ROWS), c0 : c0 + LANES] = value
                weighted[pl.ds(q0, ROWS), c0 : c0 + LANES] = (
                    tail_e[pl.ds(q0, ROWS), c0 : c0 + LANES] * value.astype(F32)
                ).astype(BF16)
            return inner

        lax.fori_loop(0, GROUP // ROWS, chunk, 0)
        fresh[pl.ds(g, 1)] = dot(
            bconv[pl.ds(r0, GROUP), 0:STATE], weighted[...], ((0,), (0,))
        )[None]
        return carry

    for load in loads[:2]:
        load.wait()
    lax.fori_loop(1, groups, states, 0)

    pl.semaphore_wait(barrier, len(partners))

    def remote(src, dst, send, recv, where):
        return pltpu.make_async_remote_copy(
            src_ref=src, dst_ref=dst, send_sem=send, recv_sem=recv,
            device_id=where, device_id_type=MESH,
        )

    halos = [
        remote(xext.at[pl.ds(length, HALO)], xext.at[pl.ds(0, HALO)], halo_s.at[0], halo_r.at[0], {"seq": following}),
        remote(bcext.at[pl.ds(length, HALO)], bcext.at[pl.ds(0, HALO)], halo_s.at[1], halo_r.at[1], {"seq": following}),
    ]
    for copy in halos:
        copy.start()

    def seg_peer(d):
        return {"seq": seg * seg_len + lax.rem(pos + d, seg_len)}

    ld_copies = []
    for d in range(1, seg_len):
        ld_copies.append(
            remote(ld_mine, ld_recv.at[pl.ds(pos, 1)], al_s.at[d - 1], al_r.at[d - 1], seg_peer(d))
        )
    for copy in ld_copies:
        copy.start()
    ld_recv[pl.ds(pos, 1)] = ld_mine[...]

    for copy in halos:
        copy.wait()
    xext[0:HALO, :] = jnp.where(me == 0, jnp.zeros((HALO, feat), BF16), xext[0:HALO, :])
    bcext[0:HALO, :] = jnp.where(me == 0, jnp.zeros((HALO, 2 * STATE), BF16), bcext[0:HALO, :])
    states(0, 0)

    group_decay = jnp.exp2(widen3(dec[...]))
    run = fresh[0]
    entry[0] = jnp.zeros((STATE, feat), F32)
    entry[1] = run
    for g in range(1, groups):
        run = group_decay[g : g + 1, :] * run + fresh[g]
        if g + 1 < groups:
            entry[g + 1] = run
    s_send[...] = run.astype(BF16).reshape(seg_len, piece, feat)

    a_copies = []
    for d in range(1, seg_len):
        to = lax.rem(pos + d, seg_len)
        a_copies.append(
            remote(s_send.at[pl.ds(to, 1)], a_recv.at[pl.ds(pos, 1)], a_s.at[d - 1], a_r.at[d - 1], seg_peer(d))
        )
    for copy in reversed(a_copies):
        copy.start()
    a_recv[pl.ds(pos, 1)] = s_send[pl.ds(pos, 1)]

    def transposes(g, carry):
        r0 = pl.multiple_of(g * GROUP, GROUP)
        ldt[pl.ds(g, 1)] = ldb[pl.ds(r0, GROUP), :].T[None, 0:16]
        stept[pl.ds(g, 1)] = stepb[pl.ds(r0, GROUP), :].T[None, 0:16]
        return carry

    skip_e = widen3(par[...])[2:3, :]

    def inside(g, carry):
        r0 = pl.multiple_of(g * GROUP, GROUP)
        scale[pl.ds(r0, GROUP), :] = widen2(jnp.exp2(ldb[pl.ds(r0, GROUP), :]))
        lane = lax.broadcasted_iota(jnp.int32, (ROWS, LANES), 1)
        for tb in range(GROUP // ROWS):
            cols = -(-(tb + 1) * ROWS // LANES) * LANES
            rt = pl.multiple_of(r0 + tb * ROWS, ROWS)
            inter = dot(
                bconv[pl.ds(rt, ROWS), STATE:], bconv[pl.ds(r0, cols), 0:STATE], ((1,), (1,))
            )
            t_i = tb * ROWS + lax.broadcasted_iota(jnp.int32, (ROWS, cols), 0)
            s_i = lax.broadcasted_iota(jnp.int32, (ROWS, cols), 1)
            keep = t_i >= s_i
            for j in range(tiles):
                c0 = j * LANES
                xs = xconv[pl.ds(r0, cols), c0 : c0 + LANES]
                halves = []
                for h in (2 * j, 2 * j + 1):
                    diff = ldb[pl.ds(rt, ROWS), h : h + 1] - ldt[g, h : h + 1, 0:cols]
                    kern = jnp.exp2(jnp.where(keep, diff, -jnp.inf))
                    mix = (inter * kern * stept[g, h : h + 1, 0:cols]).astype(BF16)
                    halves.append(dot(mix, xs))
                intra = jnp.where(lane < HEADDIM, halves[0], halves[1])
                x_t = xconv[pl.ds(rt, ROWS), c0 : c0 + LANES].astype(F32)
                gate = silu(gbuf[pl.ds(rt, ROWS), c0 : c0 + LANES].astype(F32))
                base[pl.ds(rt, ROWS), c0 : c0 + LANES] = (intra + skip_e[:, c0 : c0 + LANES] * x_t) * gate
                scale[pl.ds(rt, ROWS), c0 : c0 + LANES] = scale[pl.ds(rt, ROWS), c0 : c0 + LANES] * gate
        return carry

    lax.fori_loop(0, groups, transposes, 0)
    loads[2].wait()
    half_groups = groups // 2
    lax.fori_loop(0, half_groups, inside, 0)

    for copy in ld_copies:
        copy.wait()
    for copy in a_copies:
        copy.wait()
    lds = jnp.concatenate([ld_recv[q] for q in range(seg_len)], axis=0)
    dec_e = jnp.exp2(widen3(lds))
    run = jnp.zeros((piece, feat), F32)
    run_d = jnp.ones((1, feat), F32)
    seg_ld = ld_recv[0]
    before = []
    for q in range(seg_len):
        loc[q] = run
        before.append(run_d)
        run = dec_e[q : q + 1, :] * run + a_recv[q].astype(F32)
        run_d = run_d * dec_e[q : q + 1, :]
        if q > 0:
            seg_ld = seg_ld + ld_recv[q]
    t_send[...] = run[None]
    lt_mine[...] = seg_ld[None]

    def later_copies(k):
        where = {"seq": lax.rem(me + k * seg_len, n_seq)}
        return [
            remote(t_send, b_recv.at[pl.ds(k - 1, 1)], b_s.at[k - 1], b_r.at[k - 1], where),
            remote(lt_mine, lt_recv.at[pl.ds(k - 1, 1)], bl_s.at[k - 1], bl_r.at[k - 1], where),
        ]

    for k in range(segs - 1, 0, -1):

        @pl.when(seg + k < segs)
        def _():
            for copy in later_copies(k):
                copy.start()

    lax.fori_loop(half_groups, groups, inside, 0)

    for k in range(1, segs):

        @pl.when(seg + k < segs)
        def _():
            for copy in later_copies(k):
                copy.wait_send()

        @pl.when(seg >= k)
        def _():
            for copy in later_copies(k):
                copy.wait_recv()

    lts = jnp.concatenate([lt_recv[k] for k in range(segs - 1)] + [jnp.zeros((8 - segs + 1, LANES), F32)], axis=0)
    far_e = jnp.exp2(widen3(lts))
    carry = jnp.zeros((piece, feat), F32)
    for k in range(segs - 1, 0, -1):
        carry = far_e[k - 1 : k, :] * carry + b_recv[k - 1]
    for q in range(seg_len):
        c_send[q] = loc[q] + before[q] * carry

    c_copies = []
    for d in range(1, seg_len):
        to = lax.rem(pos + d, seg_len)
        c_copies.append(
            remote(c_send.at[pl.ds(to, 1)], inc.at[pl.ds(pos, 1)], c_s.at[d - 1], c_r.at[d - 1], seg_peer(d))
        )
    for copy in reversed(c_copies):
        copy.start()
    inc[pl.ds(pos, 1)] = c_send[pl.ds(pos, 1)]
    for copy in c_copies:
        copy.wait()

    run_d = jnp.ones((1, feat), F32)
    ss = jnp.zeros((8, LANES), F32)
    blocks = GROUP // 8
    lane8 = lax.broadcasted_iota(jnp.int32, (blocks, 8, LANES), 2)
    block_i = lax.broadcasted_iota(jnp.int32, (blocks, 8, LANES), 0)
    for g in range(groups):
        r0 = g * GROUP
        state = entry[g] + run_d * inc[...].reshape(STATE, feat)
        high, low = two_parts(state)
        c_rows = bconv[r0 : r0 + GROUP, STATE:]
        squares = jnp.zeros((GROUP, LANES), F32)
        for j in range(tiles):
            c0 = j * LANES
            carried = dot(c_rows, high[:, c0 : c0 + LANES]) + dot(c_rows, low[:, c0 : c0 + LANES])
            gated = base[r0 : r0 + GROUP, c0 : c0 + LANES] + scale[r0 : r0 + GROUP, c0 : c0 + LANES] * carried
            base[r0 : r0 + GROUP, c0 : c0 + LANES] = gated
            squares = squares + gated * gated
        total = jnp.broadcast_to(jnp.sum(squares, axis=1, keepdims=True), (GROUP, LANES))
        total = total.reshape(blocks, 8, LANES)
        ss = ss + jnp.sum(jnp.where(lane8 == block_i + g * blocks, total, 0.0), axis=0)
        run_d = run_d * group_decay[g : g + 1, :]
    ss_mine[...] = ss[None]

    x_copies = []
    for d in range(1, n_head):
        x_copies.append(
            remote(ss_mine, ss_recv.at[pl.ds(mine_h, 1)], x_s.at[d - 1], x_r.at[d - 1], {"head": lax.rem(mine_h + d, n_head)})
        )
    for copy in x_copies:
        copy.start()
    ss_recv[pl.ds(mine_h, 1)] = ss_mine[...]
    for copy in x_copies:
        copy.wait()
    ss = ss_recv[0]
    for h in range(1, n_head):
        ss = ss + ss_recv[h]
    inv = lax.rsqrt(ss * (1.0 / di) + norm_eps)
    for g in range(groups):
        spread = jnp.where(lane8 == block_i + g * blocks, jnp.broadcast_to(inv[None], (blocks, 8, LANES)), 0.0)
        row_inv = jnp.sum(spread.reshape(GROUP, LANES), axis=1, keepdims=True)
        r0 = g * GROUP
        for j in range(tiles):
            c0 = j * LANES
            out_ref[r0 : r0 + GROUP, c0 : c0 + LANES] = (
                base[r0 : r0 + GROUP, c0 : c0 + LANES] * row_inv * gain_ref[:, c0 : c0 + LANES]
            ).astype(BF16)


def on_device(n_seq, n_head, *args):
    (x_raw, bc_raw, gate_in, step_raw, cxw, cxb, cbw, cbb, dt_bias, a_log, d_skip, gain) = args
    length, feat = x_raw.shape[1], x_raw.shape[2]
    heads = dt_bias.shape[0]
    seg_len = SEG if n_seq % SEG == 0 else n_seq
    segs = n_seq // seg_len
    piece = STATE // seg_len
    groups = length // GROUP
    far = max(segs - 1, 1)
    vmem = pl.BlockSpec(memory_space=pltpu.VMEM)
    hbm = pl.BlockSpec(memory_space=pl.ANY)
    dma = pltpu.SemaphoreType.DMA
    scratch = [
        pltpu.VMEM((HALO + length, feat), BF16),
        pltpu.VMEM((HALO + length, 2 * STATE), BF16),
        pltpu.VMEM((length, feat), BF16),
        pltpu.VMEM((length, feat), BF16),
        pltpu.VMEM((length, 2 * STATE), BF16),
        pltpu.VMEM((length, LANES), F32),
        pltpu.VMEM((length, LANES), F32),
        pltpu.VMEM((groups, 16, GROUP), F32),
        pltpu.VMEM((groups, 16, GROUP), F32),
        pltpu.VMEM((8, LANES), F32),
        pltpu.VMEM((8, feat + 2 * STATE), F32),
        pltpu.VMEM((LANES, feat), BF16),
        pltpu.VMEM((GROUP, GROUP), BF16),
        pltpu.VMEM((GROUP, feat), F32),
        pltpu.VMEM((GROUP, feat), BF16),
        pltpu.VMEM((groups, STATE, feat), F32),
        pltpu.VMEM((groups, STATE, feat), F32),
        pltpu.VMEM((length, feat), F32),
        pltpu.VMEM((length, feat), F32),
        pltpu.VMEM((8, LANES), F32),
        pltpu.VMEM((seg_len, piece, feat), BF16),
        pltpu.VMEM((seg_len, piece, feat), BF16),
        pltpu.VMEM((1, 1, LANES), F32),
        pltpu.VMEM((seg_len, 1, LANES), F32),
        pltpu.VMEM((seg_len, piece, feat), F32),
        pltpu.VMEM((1, piece, feat), F32),
        pltpu.VMEM((far, piece, feat), F32),
        pltpu.VMEM((1, 1, LANES), F32),
        pltpu.VMEM((far, 1, LANES), F32),
        pltpu.VMEM((seg_len, piece, feat), F32),
        pltpu.VMEM((seg_len, piece, feat), F32),
        pltpu.VMEM((1, 8, LANES), F32),
        pltpu.VMEM((n_head, 8, LANES), F32),
        dma((3,)),
        dma((2,)), dma((2,)),
        dma((seg_len,)), dma((seg_len,)),
        dma((seg_len,)), dma((seg_len,)),
        dma((far,)), dma((far,)),
        dma((far,)), dma((far,)),
        dma((seg_len,)), dma((seg_len,)),
        dma((n_head,)), dma((n_head,)),
    ]
    sizes = (n_seq, n_head, seg_len, length, feat, heads)
    out = pl.pallas_call(
        functools.partial(kernel, sizes),
        out_shape=jax.ShapeDtypeStruct((length, feat), BF16),
        in_specs=[hbm, hbm, hbm] + [vmem] * 9,
        out_specs=vmem,
        scratch_shapes=scratch,
        compiler_params=pltpu.CompilerParams(
            collective_id=0, has_side_effects=True, vmem_limit_bytes=60 * 1024 * 1024
        ),
        name="ssd_layer",
    )(
        x_raw[0], bc_raw[0], gate_in[0], step_raw[0], cxw, cxb[None], cbw, cbb[None],
        dt_bias[None], a_log[None], d_skip[None], gain[None],
    )
    return out[None]


def solution(mesh):
    in_specs = (
        P(("member", "rep"), "seq", "head"),
        P(("member", "rep"), "seq", None),
        P(("member", "rep"), "seq", "head"),
        P(("member", "rep"), "seq", "head"),
        P("member", "head"),
        P(("member", "head")),
        P("member", None),
        P("member"),
        P(("member", "head")),
        P(("member", "head")),
        P(("member", "head")),
        P(("member", "head")),
    )
    out_specs = P(("member", "rep"), "seq", "head")
    return jax.shard_map(
        functools.partial(on_device, mesh.shape["seq"], mesh.shape["head"]),
        mesh=mesh, in_specs=in_specs, out_specs=out_specs, check_vma=False,
    )
```

time: 302 us -> 102 us (0.34)
  blocking collectives: 104 us -> 0 us
  Pallas kernels: 0 us -> 94.1 us
  waiting for transfers between devices: 70.4 us -> 0 us
  other arithmetic: 57.4 us -> 0 us
  local copies, waits for them, and re-layouts: 33.2 us -> 8.05 us
  matrix products: 15.2 us -> 0 us
  between operations: 14.4 us -> 0.01 us
  starting transfers between devices: 4.71 us -> 0 us
    pallas_call x0 -> x1, Pallas kernels: none -> 94.1 us  [on_device(): pl.pallas_call(functools.partial(kernel, sizes), out_shape=jax.ShapeDtype...]
    unnamed x1 -> x0, blocking collectives: 93.7 us -> none
    all_gather x1 -> x0, waiting for transfers between devices: 70.4 us -> none  [carried_in_2(): pieces = jax.tree.map(lambda part: lax.all_gather(part, axis), value)]
    select_n x31 -> x0, other arithmetic: 33.5 us -> none  [step(): jnp.where(position < mine, new, old)]
    dot_general x5 -> x0, matrix products: 15.2 us -> none  [the longest x1 6.92 us: on_device(): jnp.einsum('chts,cshp->cthp', mixing, x_heads, preferred_element_type=jnp...]
    psum x1 -> x0, blocking collectives: 10.2 us -> none  [on_device(): lax.psum(jnp.sum(gated_rows * gated_rows, axis=1, keepdims=True), 'head')]
    convert_element_type x7 -> x0, other arithmetic: 9.29 us -> none  [the longest x1 3.94 us: on_device(): (gated_rows * lax.rsqrt(mean_square + norm_eps) * norm_gain).astype(jnp.b...]
    dynamic_update_slice x4 -> x0, local copies, waits for them, and re-layouts: 5.19 us -> none  [on_device(): lax.scan(advance, (zero_state, jnp.ones((heads_local,), jnp.float32)), (g...]
  transfers between devices with their start and end apart: 2 -> 0, of which waited for: 1 -> 0; matrix products, arithmetic and copies ran while one was open for 8% -> 0% of each run, Pallas kernels for 0% -> 0%
where the time goes in v1:
time: 102 us
  Pallas kernels  94.1 us (92%)
  local copies, waits for them, and re-layouts  8.05 us (8%)
    pallas_call x1, Pallas kernels, on_device(): pl.pallas_call(functools.partial(kernel, sizes), out_shape=jax.ShapeDtype...  94.1 us
    unnamed x2, local copies, waits for them, and re-layouts  4.28 us

profile of v1, /device:TPU:40, one launch (start us, length us, event | category | flops | bytes accessed | tf_op | source)
XLA Modules:
  0.0 102.1 jit_solution(12519271944891356727)
XLA Ops:
  0.0 1.2 %broadcast_in_dim.22.refs_7_ = bf16[1,256]{1,0:T(2,128)(2,1)} reshape(bf16[256]{0:T(256)(128)(2,1)} %param.19) | data formatting | bytes 1024 | tf_op jit(solution)/shard_map/broadcast_in_dim | solution.py:461
  1.2 1.3 %broadcast_in_dim.21.refs_5_ = bf16[1,640]{1,0:T(2,128)(2,1)} reshape(bf16[640]{0:T(1024)(128)(2,1)} %param.17) | data formatting | bytes 2560 | tf_op jit(solution)/shard_map/broadcast_in_dim | solution.py:461
  2.5 1.3 %broadcast_in_dim.26.refs_11_ = f32[1,640]{1,0:T(1,128)} reshape(f32[640]{0:T(1024)} %param.23) | data formatting | bytes 5120 | tf_op jit(solution)/shard_map/broadcast_in_dim | solution.py:462
  3.8 1.8 %copy.13 = f32[1,1024,10]{2,1,0:T(8,128)} copy(f32[1,1024,10]{1,0,2:T(1,128)} %param.15) | data formatting | bytes 81920 | tf_op args[3]
  5.6 94.1 %ssd_layer.1 = bf16[1024,640]{1,0:T(8,128)(2,1)} custom-call(bf16[1024,640]{1,0:T(8,128)(2,1)} %bitcast.10, bf16[1024,256]{1,0:T(8,128)(2,1)} %bitcast.12, bf16[1024,640]{1,0:T(8,128)(2,1)} %bitcast.11, f32[1024,10]{1,0:T(8,128)} %bitcast.9, bf16[4,640]{1,0:T(4,128)(2,1)} %refs_4_.1, bf16[1,640]{1,0:T(2,128)(2,1)} %broadcast_in_dim.21.refs_5_, ...), custom_call_target="tpu_custom_call" | custom-call | tf_op jit(solution)/shard_map/ssd_layer/pallas_call | solution.py:450
  99.7 2.5 %copy.15 = bf16[1,1024,640]{2,1,0:T(8,128)(2,1)} copy(bf16[1,1024,640]{2,1,0:T(8,128)(2,1)} %bitcast.8) | data formatting | bytes 2621440

commit v2 on v1

--- a/solution.py
+++ b/solution.py
@@ -14,7 +14,8 @@
 LANES = 128
 HALO = 16
 ROWS = 64
-SEG = 8
+SEG = 4
+VMEM_LIMIT = 30 * 1024 * 1024
 LOG2E = 1.4426950408889634
 norm_eps = 1e-05
 
@@ -47,12 +48,13 @@
 def kernel(sizes, *refs):
     n_seq, n_head, seg_len, length, feat, heads = sizes
     (
-        x_hbm, bc_hbm, gate_hbm, step_ref, cxw_ref, cxb_ref, cbw_ref, cbb_ref,
-        dt_ref, alog_ref, skip_ref, gain_ref, out_ref,
-        xext, bcext, gbuf, xconv, bconv, stepb, ldb, ldt, stept, par, cw, expand_m, tri_m,
-        tail_e, weighted, fresh, entry, base, scale, dec,
+        x_hbm, bc_hbm, gate_hbm, step_hbm, cxw_hbm, cxb_hbm, cbw_hbm, cbb_hbm,
+        dt_hbm, alog_hbm, skip_hbm, base,
+        step_ref, cxw_ref, cxb_ref, cbw_ref, cbb_ref, dt_ref, alog_ref, skip_ref,
+        xext, bcext, gbuf, xconv, bconv, raw_t, stepb, ldb, ldt, stept, par, cw, expand_m, tri_m,
+        tail_e, weighted, fresh, entry, scale, dec,
         s_send, a_recv, ld_mine, ld_recv, loc, t_send, b_recv, lt_mine, lt_recv, c_send, inc,
-        ss_mine, ss_recv,
+        ss_mine, ss_recv, ready_h, ready_a, ready_b,
         loc_sem, halo_s, halo_r, a_s, a_r, al_s, al_r, b_s, b_r, bl_s, bl_r, c_s, c_r, x_s, x_r,
     ) = refs
     groups = length // GROUP
@@ -70,23 +72,44 @@
         pltpu.make_async_copy(x_hbm, xext.at[pl.ds(HALO, length)], loc_sem.at[0]),
         pltpu.make_async_copy(bc_hbm, bcext.at[pl.ds(HALO, length)], loc_sem.at[1]),
         pltpu.make_async_copy(gate_hbm, gbuf, loc_sem.at[2]),
+        pltpu.make_async_copy(step_hbm, step_ref, loc_sem.at[3]),
+        pltpu.make_async_copy(cxw_hbm, cxw_ref, loc_sem.at[4]),
+        pltpu.make_async_copy(cxb_hbm, cxb_ref, loc_sem.at[5]),
+        pltpu.make_async_copy(cbw_hbm, cbw_ref, loc_sem.at[6]),
+        pltpu.make_async_copy(cbb_hbm, cbb_ref, loc_sem.at[7]),
+        pltpu.make_async_copy(dt_hbm, dt_ref, loc_sem.at[8]),
+        pltpu.make_async_copy(alog_hbm, alog_ref, loc_sem.at[9]),
+        pltpu.make_async_copy(skip_hbm, skip_ref, loc_sem.at[10]),
     ]
-    for load in loads:
+    for load in loads[3:] + loads[:3]:
         load.start()
 
     b_recv[...] = jnp.zeros_like(b_recv)
     lt_recv[...] = jnp.zeros_like(lt_recv)
+    inc[...] = jnp.zeros_like(inc)
     barrier = pltpu.get_barrier_semaphore()
-    following = lax.rem(me + 1, n_seq)
-    partners = [{"seq": following}, {"seq": lax.rem(me + n_seq - 1, n_seq)}]
+
+    def greet(where):
+        pl.semaphore_signal(barrier, inc=1, device_id=where, device_id_type=MESH)
+
+    @pl.when(me + 1 < n_seq)
+    def _():
+        greet({"seq": me + 1})
+
     for d in range(1, seg_len):
-        partners.append({"seq": seg * seg_len + lax.rem(pos + d, seg_len)})
+
+        @pl.when(pos + d < seg_len)
+        def _():
+            greet({"seq": me + d})
+
     for k in range(1, segs):
-        partners.append({"seq": lax.rem(me + k * seg_len, n_seq)})
+
+        @pl.when(seg + k < segs)
+        def _():
+            greet({"seq": me + k * seg_len})
+
     for d in range(1, n_head):
-        partners.append({"head": lax.rem(mine_h + d, n_head)})
-    for partner in partners:
-        pl.semaphore_signal(barrier, inc=1, device_id=partner, device_id_type=MESH)
+        greet({"head": lax.rem(mine_h + d, n_head)})
 
     row_i = lax.broadcasted_iota(jnp.int32, (GROUP, GROUP), 0)
     col_i = lax.broadcasted_iota(jnp.int32, (GROUP, GROUP), 1)
@@ -94,14 +117,16 @@
     head_i = lax.broadcasted_iota(jnp.int32, (LANES, feat), 0)
     feat_i = lax.broadcasted_iota(jnp.int32, (LANES, feat), 1)
     expand_m[...] = jnp.where((feat_i >> 6) == head_i, 1.0, 0.0).astype(BF16)
+    for load in loads[3:]:
+        load.wait()
     par[...] = jnp.zeros_like(par)
     par[0:1, 0:heads] = dt_ref[...]
     par[1:2, 0:heads] = alog_ref[...]
     par[2:3, 0:heads] = skip_ref[...]
     cw[0:CONV, 0:feat] = cxw_ref[...].astype(F32)
-    cw[CONV : CONV + 1, 0:feat] = cxb_ref[...].astype(F32)
+    cw[CONV : CONV + 1, 0:feat] = cxb_ref[...].astype(F32).reshape(1, feat)
     cw[0:CONV, feat:] = cbw_ref[...].astype(F32)
-    cw[CONV : CONV + 1, feat:] = cbb_ref[...].astype(F32)
+    cw[CONV : CONV + 1, feat:] = cbb_ref[...].astype(F32).reshape(1, 2 * STATE)
 
     def widen3(v):
         total = None
@@ -114,13 +139,14 @@
         high, low = two_parts(v)
         return dot(high, expand_m[...]) + dot(low, expand_m[...])
 
-    stepb[...] = jnp.zeros_like(stepb)
-    stepb[:, 0:heads] = step_ref[...]
+    raw_t[...] = jnp.zeros_like(raw_t)
+    for h in range(heads):
+        raw_t[h : h + 1, :] = step_ref[h]
     rate = -LOG2E * jnp.exp(par[1:2, :])
 
     def decays(g, carry):
         r0 = pl.multiple_of(g * GROUP, GROUP)
-        raw = stepb[pl.ds(r0, GROUP), :] + par[0:1, :]
+        raw = raw_t[:, pl.ds(r0, GROUP)].T + par[0:1, :]
         step = jnp.maximum(raw, 0.0) + jnp.log1p(jnp.exp(-jnp.abs(raw)))
         stepb[pl.ds(r0, GROUP), :] = step
         total = None
@@ -180,7 +206,22 @@
         load.wait()
     lax.fori_loop(1, groups, states, 0)
 
-    pl.semaphore_wait(barrier, len(partners))
+    @pl.when(me > 0)
+    def _():
+        pl.semaphore_wait(barrier, 1 + pos + seg + n_head - 1)
+        pl.semaphore_signal(ready_h, inc=1, device_id={"seq": me - 1}, device_id_type=MESH)
+
+    for d in range(1, seg_len):
+
+        @pl.when(pos >= d)
+        def _():
+            pl.semaphore_signal(ready_a.at[d - 1], inc=1, device_id={"seq": me - d}, device_id_type=MESH)
+
+    for k in range(1, segs):
+
+        @pl.when(seg >= k)
+        def _():
+            pl.semaphore_signal(ready_b.at[k - 1], inc=1, device_id={"seq": me - k * seg_len}, device_id_type=MESH)
 
     def remote(src, dst, send, recv, where):
         return pltpu.make_async_remote_copy(
@@ -189,14 +230,24 @@
         )
 
     halos = [
-        remote(xext.at[pl.ds(length, HALO)], xext.at[pl.ds(0, HALO)], halo_s.at[0], halo_r.at[0], {"seq": following}),
-        remote(bcext.at[pl.ds(length, HALO)], bcext.at[pl.ds(0, HALO)], halo_s.at[1], halo_r.at[1], {"seq": following}),
+        remote(xext.at[pl.ds(length, HALO)], xext.at[pl.ds(0, HALO)], halo_s.at[0], halo_r.at[0], {"seq": lax.rem(me + 1, n_seq)}),
+        remote(bcext.at[pl.ds(length, HALO)], bcext.at[pl.ds(0, HALO)], halo_s.at[1], halo_r.at[1], {"seq": lax.rem(me + 1, n_seq)}),
     ]
-    for copy in halos:
-        copy.start()
+
+    @pl.when(me + 1 < n_seq)
+    def _():
+        pl.semaphore_wait(ready_h, 1)
+        for copy in halos:
+            copy.start()
 
     def seg_peer(d):
         return {"seq": seg * seg_len + lax.rem(pos + d, seg_len)}
+
+    for d in range(1, seg_len):
+
+        @pl.when(pos + d < seg_len)
+        def _():
+            pl.semaphore_wait(ready_a.at[d - 1], 1)
 
     ld_copies = []
     for d in range(1, seg_len):
@@ -207,10 +258,16 @@
         copy.start()
     ld_recv[pl.ds(pos, 1)] = ld_mine[...]
 
-    for copy in halos:
-        copy.wait()
-    xext[0:HALO, :] = jnp.where(me == 0, jnp.zeros((HALO, feat), BF16), xext[0:HALO, :])
-    bcext[0:HALO, :] = jnp.where(me == 0, jnp.zeros((HALO, 2 * STATE), BF16), bcext[0:HALO, :])
+    @pl.when(me > 0)
+    def _():
+        for copy in halos:
+            copy.wait_recv()
+
+    @pl.when(me == 0)
+    def _():
+        xext[0:HALO, :] = jnp.zeros((HALO, feat), BF16)
+        bcext[0:HALO, :] = jnp.zeros((HALO, 2 * STATE), BF16)
+
     states(0, 0)
 
     group_decay = jnp.exp2(widen3(dec[...]))
@@ -272,8 +329,7 @@
 
     lax.fori_loop(0, groups, transposes, 0)
     loads[2].wait()
-    half_groups = groups // 2
-    lax.fori_loop(0, half_groups, inside, 0)
+    lax.fori_loop(0, jnp.where(me == 0, 0, groups), inside, 0)
 
     for copy in ld_copies:
         copy.wait()
@@ -302,21 +358,15 @@
             remote(lt_mine, lt_recv.at[pl.ds(k - 1, 1)], bl_s.at[k - 1], bl_r.at[k - 1], where),
         ]
 
-    for k in range(segs - 1, 0, -1):
+    for k in range(1, segs):
 
         @pl.when(seg + k < segs)
         def _():
+            pl.semaphore_wait(ready_b.at[k - 1], 1)
             for copy in later_copies(k):
                 copy.start()
 
-    lax.fori_loop(half_groups, groups, inside, 0)
-
     for k in range(1, segs):
-
-        @pl.when(seg + k < segs)
-        def _():
-            for copy in later_copies(k):
-                copy.wait_send()
 
         @pl.when(seg >= k)
         def _():
@@ -334,14 +384,21 @@
     c_copies = []
     for d in range(1, seg_len):
         to = lax.rem(pos + d, seg_len)
-        c_copies.append(
-            remote(c_send.at[pl.ds(to, 1)], inc.at[pl.ds(pos, 1)], c_s.at[d - 1], c_r.at[d - 1], seg_peer(d))
-        )
-    for copy in reversed(c_copies):
-        copy.start()
+        copy = remote(c_send.at[pl.ds(to, 1)], inc.at[pl.ds(pos, 1)], c_s.at[d - 1], c_r.at[d - 1], seg_peer(d))
+        c_copies.append((seg + to > 0, copy))
+    for wanted, copy in c_copies:
+
+        @pl.when(wanted)
+        def _():
+            copy.start()
+
     inc[pl.ds(pos, 1)] = c_send[pl.ds(pos, 1)]
-    for copy in c_copies:
-        copy.wait()
+    lax.fori_loop(0, jnp.where(me == 0, groups, 0), inside, 0)
+
+    @pl.when(me > 0)
+    def _():
+        for _, copy in c_copies:
+            copy.wait_recv()
 
     run_d = jnp.ones((1, feat), F32)
     ss = jnp.zeros((8, LANES), F32)
@@ -366,6 +423,10 @@
         run_d = run_d * group_decay[g : g + 1, :]
     ss_mine[...] = ss[None]
 
+    @pl.when(me == 0)
+    def _():
+        pl.semaphore_wait(barrier, n_head - 1)
+
     x_copies = []
     for d in range(1, n_head):
         x_copies.append(
@@ -386,9 +447,25 @@
         r0 = g * GROUP
         for j in range(tiles):
             c0 = j * LANES
-            out_ref[r0 : r0 + GROUP, c0 : c0 + LANES] = (
-                base[r0 : r0 + GROUP, c0 : c0 + LANES] * row_inv * gain_ref[:, c0 : c0 + LANES]
-            ).astype(BF16)
+            base[r0 : r0 + GROUP, c0 : c0 + LANES] = base[r0 : r0 + GROUP, c0 : c0 + LANES] * row_inv
+
+    @pl.when(me + 1 < n_seq)
+    def _():
+        for copy in halos:
+            copy.wait_send()
+
+    for k in range(1, segs):
+
+        @pl.when(seg + k < segs)
+        def _():
+            for copy in later_copies(k):
+                copy.wait_send()
+
+    for wanted, copy in c_copies:
+
+        @pl.when(wanted)
+        def _():
+            copy.wait_send()
 
 
 def on_device(n_seq, n_head, *args):
@@ -401,14 +478,24 @@
     groups = length // GROUP
     far = max(segs - 1, 1)
     vmem = pl.BlockSpec(memory_space=pltpu.VMEM)
-    hbm = pl.BlockSpec(memory_space=pl.ANY)
+    hbm = pl.BlockSpec(memory_space=pltpu.HBM)
     dma = pltpu.SemaphoreType.DMA
+    regular = pltpu.SemaphoreType.REGULAR
     scratch = [
+        pltpu.VMEM((heads, 1, length), F32),
+        pltpu.VMEM((CONV, feat), BF16),
+        pltpu.VMEM((feat,), BF16),
+        pltpu.VMEM((CONV, 2 * STATE), BF16),
+        pltpu.VMEM((2 * STATE,), BF16),
+        pltpu.VMEM((1, heads), F32),
+        pltpu.VMEM((1, heads), F32),
+        pltpu.VMEM((1, heads), F32),
         pltpu.VMEM((HALO + length, feat), BF16),
         pltpu.VMEM((HALO + length, 2 * STATE), BF16),
         pltpu.VMEM((length, feat), BF16),
         pltpu.VMEM((length, feat), BF16),
         pltpu.VMEM((length, 2 * STATE), BF16),
+        pltpu.VMEM((LANES, length), F32),
         pltpu.VMEM((length, LANES), F32),
         pltpu.VMEM((length, LANES), F32),
         pltpu.VMEM((groups, 16, GROUP), F32),
@@ -421,7 +508,6 @@
         pltpu.VMEM((GROUP, feat), BF16),
         pltpu.VMEM((groups, STATE, feat), F32),
         pltpu.VMEM((groups, STATE, feat), F32),
-        pltpu.VMEM((length, feat), F32),
         pltpu.VMEM((length, feat), F32),
         pltpu.VMEM((8, LANES), F32),
         pltpu.VMEM((seg_len, piece, feat), BF16),
@@ -437,7 +523,8 @@
         pltpu.VMEM((seg_len, piece, feat), F32),
         pltpu.VMEM((1, 8, LANES), F32),
         pltpu.VMEM((n_head, 8, LANES), F32),
-        dma((3,)),
+        regular, regular((seg_len,)), regular((far,)),
+        dma((11,)),
         dma((2,)), dma((2,)),
         dma((seg_len,)), dma((seg_len,)),
         dma((seg_len,)), dma((seg_len,)),
@@ -449,19 +536,19 @@
     sizes = (n_seq, n_head, seg_len, length, feat, heads)
     out = pl.pallas_call(
         functools.partial(kernel, sizes),
-        out_shape=jax.ShapeDtypeStruct((length, feat), BF16),
-        in_specs=[hbm, hbm, hbm] + [vmem] * 9,
+        out_shape=jax.ShapeDtypeStruct((length, feat), F32),
+        in_specs=[hbm] * 11,
         out_specs=vmem,
         scratch_shapes=scratch,
         compiler_params=pltpu.CompilerParams(
-            collective_id=0, has_side_effects=True, vmem_limit_bytes=60 * 1024 * 1024
+            collective_id=0, has_side_effects=True, vmem_limit_bytes=VMEM_LIMIT
         ),
         name="ssd_layer",
     )(
-        x_raw[0], bc_raw[0], gate_in[0], step_raw[0], cxw, cxb[None], cbw, cbb[None],
-        dt_bias[None], a_log[None], d_skip[None], gain[None],
+        x_raw[0], bc_raw[0], gate_in[0], jnp.transpose(step_raw, (2, 0, 1)), cxw, cxb, cbw, cbb,
+        dt_bias[None], a_log[None], d_skip[None],
     )
-    return out[None]
+    return (out * gain).astype(BF16)[None]
 
 
 def solution(mesh):

time: 102 us -> 117 us (1.15)
  the two profiles are of different devices: /device:TPU:40 before, /device:TPU:46 now
where the time goes in v2:
time: 117 us; the launch traced here: 116 us
  Pallas kernels  106 us (91%)
  local copies, waits for them, and re-layouts  9.12 us (8%)
  other arithmetic  1.27 us (1%)
    pallas_call x1, Pallas kernels, on_device(): pl.pallas_call(functools.partial(kernel, sizes), out_shape=jax.ShapeDtype...  106 us
    unnamed x24, local copies, waits for them, and re-layouts  9.12 us

profile of v2, /device:TPU:46, one launch (start us, length us, event | category | flops | bytes accessed | tf_op | source)
XLA Modules:
  0.0 116.3 jit_solution(7944858412525029546)
XLA Ops:
  0.0 0.0 copy-start
  0.0 1.3 %copy-done = bf16[1,1024,640]{2,1,0:T(8,128)(2,1)S(1)} copy-done((bf16[1,1024,640]{2,1,0:T(8,128)(2,1)S(1)}, bf16[1,1024,640]{2,1,0:T(8,128)(2,1)}, u32[]{:S(2)}) %copy-start) | copy-done | bytes 1310744
  1.3 0.0 copy-start.1
  1.3 1.3 %copy-done.1 = bf16[1,1024,640]{2,1,0:T(8,128)(2,1)S(1)} copy-done((bf16[1,1024,640]{2,1,0:T(8,128)(2,1)S(1)}, bf16[1,1024,640]{2,1,0:T(8,128)(2,1)}, u32[]{:S(2)}) %copy-start.1) | copy-done | bytes 1310744
  2.6 0.0 copy-start.2
  2.6 1.0 copy-done.2
  3.7 0.0 copy-start.3
  3.7 0.8 copy-done.3
  4.5 0.0 copy-start.4
  4.5 0.7 copy-done.4
  5.1 0.0 copy-start.5
  5.1 0.7 copy-done.5
  5.8 0.0 copy-start.6
  5.8 0.7 copy-done.6
  6.5 0.0 copy-start.7
  6.5 0.7 copy-done.7
  7.2 0.0 copy-start.8
  7.2 0.7 copy-done.8
  7.8 0.0 copy-start.9
  7.8 0.7 copy-done.9
  8.5 0.0 copy-start.10
  8.5 0.7 copy-done.10
  9.1 0.0 copy-start.11
  9.1 105.9 %ssd_layer.1 = f32[1024,640]{1,0:T(8,128)S(1)} custom-call(bf16[1024,640]{1,0:T(8,128)(2,1)S(1)} %bitcast.9, bf16[1024,256]{1,0:T(8,128)(2,1)S(1)} %bitcast.11, bf16[1024,640]{1,0:T(8,128)(2,1)S(1)} %bitcast.10, f32[10,1,1024]{2,1,0:T(1,128)S(1)} %bitcast.12, bf16[4,640]{1,0:T(4,128)(2,1)S(1)} %copy-done.4, bf16[640]{0:T(1024)(128)(2,1)S(1)} %copy-done.5, ...), custom_call_target="tpu_custom_call" | custom-call | tf_op jit(solution)/shard_map/ssd_layer/pallas_call | solution.py:537
  115.1 0.0 copy-done.11
  115.1 1.3 %fusion = bf16[1,1024,640]{2,1,0:T(8,128)(2,1)} fusion(f32[1024,640]{1,0:T(8,128)S(1)} %ssd_layer.1, f32[640]{0:T(1024)S(1)} %copy-done.11), kind=kLoop, calls=%fused_computation.1 | loop fusion | flops 1310720 | bytes 3934720 | tf_op jit(solution)/shard_map/broadcast_in_dim | solution.py:551
Async XLA Ops:
  0.0 1.3 %copy-start = (bf16[1,1024,640]{2,1,0:T(8,128)(2,1)S(1)}, bf16[1,1024,640]{2,1,0:T(8,128)(2,1)}, u32[]{:S(2)}) copy-start(bf16[1,1024,640]{2,1,0:T(8,128)(2,1)} %param.12) | copy-start | bytes 3932164
  1.3 1.3 %copy-start.1 = (bf16[1,1024,640]{2,1,0:T(8,128)(2,1)S(1)}, bf16[1,1024,640]{2,1,0:T(8,128)(2,1)}, u32[]{:S(2)}) copy-start(bf16[1,1024,640]{2,1,0:T(8,128)(2,1)} %param.14) | copy-start | bytes 3932164
  2.6 1.0 copy-start.2
  3.7 0.8 copy-start.3
  4.5 0.7 copy-start.4
  5.1 0.7 copy-start.5
  5.8 0.7 copy-start.6
  6.5 0.7 copy-start.7
  7.2 0.7 copy-start.8
  7.8 0.7 copy-start.9
  8.5 0.7 copy-start.10
  9.1 105.9 %copy-start.11 = (f32[640]{0:T(1024)S(1)}, f32[640]{0:T(1024)}, u32[]{:S(2)}) copy-start(f32[640]{0:T(1024)} %param.23) | copy-start | bytes 7684

commit v3 on v2

--- a/solution.py
+++ b/solution.py
@@ -53,9 +53,9 @@
         step_ref, cxw_ref, cxb_ref, cbw_ref, cbb_ref, dt_ref, alog_ref, skip_ref,
         xext, bcext, gbuf, xconv, bconv, raw_t, stepb, ldb, ldt, stept, par, cw, expand_m, tri_m,
         tail_e, weighted, fresh, entry, scale, dec,
-        s_send, a_recv, ld_mine, ld_recv, loc, t_send, b_recv, lt_mine, lt_recv, c_send, inc,
+        s_send, a_recv, ld_mine, ld_recv, loc, t_send, b_recv, c_send, inc,
         ss_mine, ss_recv, ready_h, ready_a, ready_b,
-        loc_sem, halo_s, halo_r, a_s, a_r, al_s, al_r, b_s, b_r, bl_s, bl_r, c_s, c_r, x_s, x_r,
+        loc_sem, halo_s, halo_r, a_s, a_r, al_s, al_r, b_s, b_r, c_s, c_r, x_s, x_r,
     ) = refs
     groups = length // GROUP
     tiles = feat // LANES
@@ -85,7 +85,6 @@
         load.start()
 
     b_recv[...] = jnp.zeros_like(b_recv)
-    lt_recv[...] = jnp.zeros_like(lt_recv)
     inc[...] = jnp.zeros_like(inc)
     barrier = pltpu.get_barrier_semaphore()
 
@@ -102,11 +101,9 @@
         def _():
             greet({"seq": me + d})
 
-    for k in range(1, segs):
-
-        @pl.when(seg + k < segs)
-        def _():
-            greet({"seq": me + k * seg_len})
+    @pl.when(seg + 1 < segs)
+    def _():
+        greet({"seq": me + seg_len})
 
     for d in range(1, n_head):
         greet({"head": lax.rem(mine_h + d, n_head)})
@@ -208,7 +205,7 @@
 
     @pl.when(me > 0)
     def _():
-        pl.semaphore_wait(barrier, 1 + pos + seg + n_head - 1)
+        pl.semaphore_wait(barrier, 1 + pos + jnp.where(seg > 0, 1, 0) + n_head - 1)
         pl.semaphore_signal(ready_h, inc=1, device_id={"seq": me - 1}, device_id_type=MESH)
 
     for d in range(1, seg_len):
@@ -217,11 +214,9 @@
         def _():
             pl.semaphore_signal(ready_a.at[d - 1], inc=1, device_id={"seq": me - d}, device_id_type=MESH)
 
-    for k in range(1, segs):
-
-        @pl.when(seg >= k)
-        def _():
-            pl.semaphore_signal(ready_b.at[k - 1], inc=1, device_id={"seq": me - k * seg_len}, device_id_type=MESH)
+    @pl.when(seg > 0)
+    def _():
+        pl.semaphore_signal(ready_b, inc=1, device_id={"seq": me - seg_len}, device_id_type=MESH)
 
     def remote(src, dst, send, recv, where):
         return pltpu.make_async_remote_copy(
@@ -339,45 +334,27 @@
     dec_e = jnp.exp2(widen3(lds))
     run = jnp.zeros((piece, feat), F32)
     run_d = jnp.ones((1, feat), F32)
-    seg_ld = ld_recv[0]
     before = []
     for q in range(seg_len):
         loc[q] = run
         before.append(run_d)
         run = dec_e[q : q + 1, :] * run + a_recv[q].astype(F32)
         run_d = run_d * dec_e[q : q + 1, :]
-        if q > 0:
-            seg_ld = seg_ld + ld_recv[q]
-    t_send[...] = run[None]
-    lt_mine[...] = seg_ld[None]
-
-    def later_copies(k):
-        where = {"seq": lax.rem(me + k * seg_len, n_seq)}
-        return [
-            remote(t_send, b_recv.at[pl.ds(k - 1, 1)], b_s.at[k - 1], b_r.at[k - 1], where),
-            remote(lt_mine, lt_recv.at[pl.ds(k - 1, 1)], bl_s.at[k - 1], bl_r.at[k - 1], where),
-        ]
-
-    for k in range(1, segs):
-
-        @pl.when(seg + k < segs)
-        def _():
-            pl.semaphore_wait(ready_b.at[k - 1], 1)
-            for copy in later_copies(k):
-                copy.start()
-
-    for k in range(1, segs):
-
-        @pl.when(seg >= k)
-        def _():
-            for copy in later_copies(k):
-                copy.wait_recv()
-
-    lts = jnp.concatenate([lt_recv[k] for k in range(segs - 1)] + [jnp.zeros((8 - segs + 1, LANES), F32)], axis=0)
-    far_e = jnp.exp2(widen3(lts))
-    carry = jnp.zeros((piece, feat), F32)
-    for k in range(segs - 1, 0, -1):
-        carry = far_e[k - 1 : k, :] * carry + b_recv[k - 1]
+
+    onward = remote(t_send, b_recv, b_s, b_r, {"seq": lax.rem(me + seg_len, n_seq)})
+
+    @pl.when(seg > 0)
+    def _():
+        onward.wait_recv()
+
+    carry = b_recv[0]
+    t_send[...] = (run + run_d * carry)[None]
+
+    @pl.when(seg + 1 < segs)
+    def _():
+        pl.semaphore_wait(ready_b, 1)
+        onward.start()
+
     for q in range(seg_len):
         c_send[q] = loc[q] + before[q] * carry
 
@@ -454,12 +431,9 @@
         for copy in halos:
             copy.wait_send()
 
-    for k in range(1, segs):
-
-        @pl.when(seg + k < segs)
-        def _():
-            for copy in later_copies(k):
-                copy.wait_send()
+    @pl.when(seg + 1 < segs)
+    def _():
+        onward.wait_send()
 
     for wanted, copy in c_copies:
 
@@ -473,10 +447,8 @@
     length, feat = x_raw.shape[1], x_raw.shape[2]
     heads = dt_bias.shape[0]
     seg_len = SEG if n_seq % SEG == 0 else n_seq
-    segs = n_seq // seg_len
     piece = STATE // seg_len
     groups = length // GROUP
-    far = max(segs - 1, 1)
     vmem = pl.BlockSpec(memory_space=pltpu.VMEM)
     hbm = pl.BlockSpec(memory_space=pltpu.HBM)
     dma = pltpu.SemaphoreType.DMA
@@ -516,24 +488,22 @@
         pltpu.VMEM((seg_len, 1, LANES), F32),
         pltpu.VMEM((seg_len, piece, feat), F32),
         pltpu.VMEM((1, piece, feat), F32),
-        pltpu.VMEM((far, piece, feat), F32),
-        pltpu.VMEM((1, 1, LANES), F32),
-        pltpu.VMEM((far, 1, LANES), F32),
+        pltpu.VMEM((1, piece, feat), F32),
         pltpu.VMEM((seg_len, piece, feat), F32),
         pltpu.VMEM((seg_len, piece, feat), F32),
         pltpu.VMEM((1, 8, LANES), F32),
         pltpu.VMEM((n_head, 8, LANES), F32),
-        regular, regular((seg_len,)), regular((far,)),
+        regular, regular((seg_len,)), regular,
         dma((11,)),
         dma((2,)), dma((2,)),
         dma((seg_len,)), dma((seg_len,)),
         dma((seg_len,)), dma((seg_len,)),
-        dma((far,)), dma((far,)),
-        dma((far,)), dma((far,)),
+        dma, dma,
         dma((seg_len,)), dma((seg_len,)),
         dma((n_head,)), dma((n_head,)),
     ]
     sizes = (n_seq, n_head, seg_len, length, feat, heads)
+    keep = lambda v: pltpu.with_memory_space_constraint(v, pltpu.HBM)
     out = pl.pallas_call(
         functools.partial(kernel, sizes),
         out_shape=jax.ShapeDtypeStruct((length, feat), F32),
@@ -545,8 +515,10 @@
         ),
         name="ssd_layer",
     )(
-        x_raw[0], bc_raw[0], gate_in[0], jnp.transpose(step_raw, (2, 0, 1)), cxw, cxb, cbw, cbb,
-        dt_bias[None], a_log[None], d_skip[None],
+        *map(keep, (
+            x_raw[0], bc_raw[0], gate_in[0], jnp.transpose(step_raw, (2, 0, 1)), cxw, cxb, cbw, cbb,
+            dt_bias[None], a_log[None], d_skip[None],
+        ))
     )
     return (out * gain).astype(BF16)[None]
 

time: 117 us -> 71.7 us (0.61)
  the two profiles are of different devices: /device:TPU:46 before, /device:TPU:1826 now
where the time goes in v3:
time: 71.7 us; the launch traced here: 71.6 us
  Pallas kernels  70.3 us (98%)
  other arithmetic  1.25 us (2%)
    pallas_call x1, Pallas kernels, on_device(): pl.pallas_call(functools.partial(kernel, sizes), out_shape=jax.ShapeDtype...  70.3 us

profile of v3, /device:TPU:1826, one launch (start us, length us, event | category | flops | bytes accessed | tf_op | source)
XLA Modules:
  0.0 71.6 jit_solution(18388989132997532810)
XLA Ops:
  0.0 0.0 copy-start
  0.0 70.3 %ssd_layer.1 = f32[1024,640]{1,0:T(8,128)S(1)} custom-call(bf16[1024,640]{1,0:T(8,128)(2,1)} %bitcast.9, bf16[1024,256]{1,0:T(8,128)(2,1)} %bitcast.11, bf16[1024,640]{1,0:T(8,128)(2,1)} %bitcast.10, f32[10,1,1024]{2,1,0:T(1,128)} %bitcast.12, bf16[4,640]{1,0:T(4,128)(2,1)} %refs_4_.1, bf16[640]{0:T(1024)(128)(2,1)} %refs_5_.1, bf16[4,256]{1,0:T(4,128)(2,1)} %refs_6_.1, ...), custom_call_target="tpu_custom_call" | custom-call | tf_op jit(solution)/shard_map/ssd_layer/pallas_call | solution.py:507
  70.3 0.0 copy-done
  70.3 1.2 %fusion = bf16[1,1024,640]{2,1,0:T(8,128)(2,1)} fusion(f32[1024,640]{1,0:T(8,128)S(1)} %ssd_layer.1, f32[640]{0:T(1024)S(1)} %copy-done), kind=kLoop, calls=%fused_computation.1 | loop fusion | flops 1310720 | bytes 3934720 | tf_op jit(solution)/shard_map/broadcast_in_dim | solution.py:523
Async XLA Ops:
  0.0 70.3 %copy-start = (f32[640]{0:T(1024)S(1)}, f32[640]{0:T(1024)}, u32[]{:S(2)}) copy-start(f32[640]{0:T(1024)} %param.23) | copy-start | bytes 7684

commit v4 on v3

--- a/solution.py
+++ b/solution.py
@@ -24,8 +24,7 @@
 MESH = pl.DeviceIdType.MESH
 
 
-def silu(v):
-    half = 0.5 * v
+def silu_of_half(half):
     return half + half * jnp.tanh(half)
 
 
@@ -51,11 +50,11 @@
         x_hbm, bc_hbm, gate_hbm, step_hbm, cxw_hbm, cxb_hbm, cbw_hbm, cbb_hbm,
         dt_hbm, alog_hbm, skip_hbm, base,
         step_ref, cxw_ref, cxb_ref, cbw_ref, cbb_ref, dt_ref, alog_ref, skip_ref,
-        xext, bcext, gbuf, xconv, bconv, raw_t, stepb, ldb, ldt, stept, par, cw, expand_m, tri_m,
+        xext, bcext, gbuf, xconv, bconv, raw_t, shifts, stepb, ldb, ldt, stept, par, cw, expand_m, tri_m,
         tail_e, weighted, fresh, entry, scale, dec,
-        s_send, a_recv, ld_mine, ld_recv, loc, t_send, b_recv, c_send, inc,
-        ss_mine, ss_recv, ready_h, ready_a, ready_b,
-        loc_sem, halo_s, halo_r, a_s, a_r, al_s, al_r, b_s, b_r, c_s, c_r, x_s, x_r,
+        s_send, a_recv, ld_mine, ld_recv, loc, t_send, b_recv, lx_mine, lx_recv, f_recv, c_send, inc,
+        ss_mine, ss_recv, ready_h, ready_a, ready_b, ready_w,
+        loc_sem, halo_s, halo_r, a_s, a_r, al_s, al_r, b_s, b_r, bl_s, bl_r, f_s, f_r, fw_s, c_s, c_r, x_s, x_r,
     ) = refs
     groups = length // GROUP
     tiles = feat // LANES
@@ -63,10 +62,13 @@
     segs = n_seq // seg_len
     di = feat * n_head
 
+    middle = segs // 2
+    wrap = segs - 1 > middle
     me = lax.axis_index("seq")
     mine_h = lax.axis_index("head")
     seg = me // seg_len
     pos = lax.rem(me, seg_len)
+    last_seg = jnp.where(seg == segs - 1, 1, 0) if wrap else 0
 
     loads = [
         pltpu.make_async_copy(x_hbm, xext.at[pl.ds(HALO, length)], loc_sem.at[0]),
@@ -85,6 +87,7 @@
         load.start()
 
     b_recv[...] = jnp.zeros_like(b_recv)
+    lx_recv[...] = jnp.zeros_like(lx_recv)
     inc[...] = jnp.zeros_like(inc)
     barrier = pltpu.get_barrier_semaphore()
 
@@ -105,71 +108,76 @@
     def _():
         greet({"seq": me + seg_len})
 
+    if wrap:
+
+        @pl.when(seg == 0)
+        def _():
+            greet({"seq": me + (segs - 1) * seg_len})
+
     for d in range(1, n_head):
         greet({"head": lax.rem(mine_h + d, n_head)})
 
     row_i = lax.broadcasted_iota(jnp.int32, (GROUP, GROUP), 0)
     col_i = lax.broadcasted_iota(jnp.int32, (GROUP, GROUP), 1)
-    tri_m[...] = jnp.where(row_i >= col_i, 1.0, 0.0).astype(BF16)
-    head_i = lax.broadcasted_iota(jnp.int32, (LANES, feat), 0)
-    feat_i = lax.broadcasted_iota(jnp.int32, (LANES, feat), 1)
-    expand_m[...] = jnp.where((feat_i >> 6) == head_i, 1.0, 0.0).astype(BF16)
+    tri_m[...] = jnp.where(row_i <= col_i, 1.0, 0.0).astype(BF16)
+    head_i = lax.broadcasted_iota(jnp.int32, (2 * LANES, feat), 0)
+    feat_i = lax.broadcasted_iota(jnp.int32, (2 * LANES, feat), 1)
+    expand_m[...] = jnp.where((feat_i >> 6) == (head_i & (LANES - 1)), 1.0, 0.0).astype(BF16)
     for load in loads[3:]:
         load.wait()
     par[...] = jnp.zeros_like(par)
     par[0:1, 0:heads] = dt_ref[...]
     par[1:2, 0:heads] = alog_ref[...]
     par[2:3, 0:heads] = skip_ref[...]
-    cw[0:CONV, 0:feat] = cxw_ref[...].astype(F32)
-    cw[CONV : CONV + 1, 0:feat] = cxb_ref[...].astype(F32).reshape(1, feat)
-    cw[0:CONV, feat:] = cbw_ref[...].astype(F32)
-    cw[CONV : CONV + 1, feat:] = cbb_ref[...].astype(F32).reshape(1, 2 * STATE)
+    cw[0:CONV, 0:feat] = 0.5 * cxw_ref[...].astype(F32)
+    cw[CONV : CONV + 1, 0:feat] = 0.5 * cxb_ref[...].astype(F32).reshape(1, feat)
+    cw[0:CONV, feat:] = 0.5 * cbw_ref[...].astype(F32)
+    cw[CONV : CONV + 1, feat:] = 0.5 * cbb_ref[...].astype(F32).reshape(1, 2 * STATE)
 
     def widen3(v):
         total = None
         for part in three_parts(v):
-            term = dot(part, expand_m[...])
+            term = dot(part, expand_m[0:LANES, :])
             total = term if total is None else total + term
         return total
 
     def widen2(v):
         high, low = two_parts(v)
-        return dot(high, expand_m[...]) + dot(low, expand_m[...])
+        return dot(jnp.concatenate([high, low], axis=1), expand_m[...])
 
     raw_t[...] = jnp.zeros_like(raw_t)
     for h in range(heads):
         raw_t[h : h + 1, :] = step_ref[h]
-    rate = -LOG2E * jnp.exp(par[1:2, :])
-
-    def decays(g, carry):
-        r0 = pl.multiple_of(g * GROUP, GROUP)
-        raw = raw_t[:, pl.ds(r0, GROUP)].T + par[0:1, :]
-        step = jnp.maximum(raw, 0.0) + jnp.log1p(jnp.exp(-jnp.abs(raw)))
-        stepb[pl.ds(r0, GROUP), :] = step
-        total = None
-        for part in three_parts(rate * step):
-            term = dot(tri_m[...], part)
-            total = term if total is None else total + term
-        ldb[pl.ds(r0, GROUP), :] = total
-        dec[pl.ds(g, 1), :] = total[GROUP - 1 : GROUP, :]
-        return carry
-
+    par_t = par[...].T
+    raw = raw_t[...] + par_t[0:16, 0:1]
+    step = jnp.maximum(raw, 0.0) + jnp.log1p(jnp.exp(-jnp.abs(raw)))
+    raw_t[...] = step
+    rates = jnp.concatenate(three_parts(-LOG2E * jnp.exp(par_t[0:16, 1:2]) * step), axis=0)
+    rest = jnp.zeros((LANES - 16, GROUP), F32)
     dec[...] = jnp.zeros_like(dec)
-    lax.fori_loop(0, groups, decays, 0)
+    for g in range(groups):
+        r0 = g * GROUP
+        sums = dot(rates[:, r0 : r0 + GROUP], tri_m[...])
+        sums = sums[0:16] + sums[16:32] + sums[32:48]
+        ldt[g] = sums
+        stept[g] = raw_t[:, r0 : r0 + GROUP]
+        ldb[r0 : r0 + GROUP, :] = jnp.concatenate([sums, rest], axis=0).T
+        stepb[r0 : r0 + GROUP, :] = jnp.concatenate([stept[g], rest], axis=0).T
+        dec[g : g + 1, :] = ldb[r0 + GROUP - 1 : r0 + GROUP, :]
     ld_total = dec[0:1, :]
     for g in range(1, groups):
         ld_total = ld_total + dec[g : g + 1, :]
     ld_mine[...] = ld_total[None]
 
-    def conv(ext, r, c0, width, tile, w_off):
-        block = ext[pl.ds(r, ROWS + HALO), c0 : c0 + width].astype(F32)
-        lo = w_off + c0
-        acc = cw[CONV : CONV + 1, lo : lo + width]
+    def conv(ext, r, j, w_off):
+        slot = j + w_off // LANES
+        shifts[slot] = ext[pl.ds(r, ROWS + HALO), j * LANES : (j + 1) * LANES].astype(F32)
+        lo = w_off + j * LANES
+        acc = cw[CONV : CONV + 1, lo : lo + LANES]
         for k in range(CONV):
-            shift = CONV - 1 - k
-            moved = block if shift == 0 else pltpu.roll(block, shift, 0)
-            acc = acc + cw[k : k + 1, lo : lo + width] * moved[HALO:]
-        return silu(acc)
+            start = HALO - (CONV - 1 - k)
+            acc = acc + cw[k : k + 1, lo : lo + LANES] * shifts[slot, start : start + ROWS, :]
+        return silu_of_half(acc)
 
     def states(g, carry):
         r0 = pl.multiple_of(g * GROUP, GROUP)
@@ -181,12 +189,10 @@
             q0 = pl.multiple_of(i * ROWS, ROWS)
             r = pl.multiple_of(r0 + q0, ROWS)
             for j in range(2 * STATE // LANES):
-                bconv[pl.ds(r, ROWS), j * LANES : (j + 1) * LANES] = conv(
-                    bcext, r, j * LANES, LANES, j, feat
-                ).astype(BF16)
+                bconv[pl.ds(r, ROWS), j * LANES : (j + 1) * LANES] = conv(bcext, r, j, feat).astype(BF16)
             for j in range(tiles):
                 c0 = j * LANES
-                value = conv(xext, r, c0, LANES, j, 0).astype(BF16)
+                value = conv(xext, r, j, 0).astype(BF16)
                 xconv[pl.ds(r, ROWS), c0 : c0 + LANES] = value
                 weighted[pl.ds(q0, ROWS), c0 : c0 + LANES] = (
                     tail_e[pl.ds(q0, ROWS), c0 : c0 + LANES] * value.astype(F32)
@@ -205,7 +211,7 @@
 
     @pl.when(me > 0)
     def _():
-        pl.semaphore_wait(barrier, 1 + pos + jnp.where(seg > 0, 1, 0) + n_head - 1)
+        pl.semaphore_wait(barrier, 1 + pos + jnp.where(seg > 0, 1, 0) + n_head - 1 + last_seg)
         pl.semaphore_signal(ready_h, inc=1, device_id={"seq": me - 1}, device_id_type=MESH)
 
     for d in range(1, seg_len):
@@ -217,6 +223,12 @@
     @pl.when(seg > 0)
     def _():
         pl.semaphore_signal(ready_b, inc=1, device_id={"seq": me - seg_len}, device_id_type=MESH)
+
+    if wrap:
+
+        @pl.when(seg == segs - 1)
+        def _():
+            pl.semaphore_signal(ready_w, inc=1, device_id={"seq": me - (segs - 1) * seg_len}, device_id_type=MESH)
 
     def remote(src, dst, send, recv, where):
         return pltpu.make_async_remote_copy(
@@ -284,12 +296,6 @@
     for copy in reversed(a_copies):
         copy.start()
     a_recv[pl.ds(pos, 1)] = s_send[pl.ds(pos, 1)]
-
-    def transposes(g, carry):
-        r0 = pl.multiple_of(g * GROUP, GROUP)
-        ldt[pl.ds(g, 1)] = ldb[pl.ds(r0, GROUP), :].T[None, 0:16]
-        stept[pl.ds(g, 1)] = stepb[pl.ds(r0, GROUP), :].T[None, 0:16]
-        return carry
 
     skip_e = widen3(par[...])[2:3, :]
 
@@ -317,12 +323,11 @@
                     halves.append(dot(mix, xs))
                 intra = jnp.where(lane < HEADDIM, halves[0], halves[1])
                 x_t = xconv[pl.ds(rt, ROWS), c0 : c0 + LANES].astype(F32)
-                gate = silu(gbuf[pl.ds(rt, ROWS), c0 : c0 + LANES].astype(F32))
+                gate = silu_of_half(0.5 * gbuf[pl.ds(rt, ROWS), c0 : c0 + LANES].astype(F32))
                 base[pl.ds(rt, ROWS), c0 : c0 + LANES] = (intra + skip_e[:, c0 : c0 + LANES] * x_t) * gate
                 scale[pl.ds(rt, ROWS), c0 : c0 + LANES] = scale[pl.ds(rt, ROWS), c0 : c0 + LANES] * gate
         return carry
 
-    lax.fori_loop(0, groups, transposes, 0)
     loads[2].wait()
     lax.fori_loop(0, jnp.where(me == 0, 0, groups), inside, 0)
 
@@ -341,20 +346,55 @@
         run = dec_e[q : q + 1, :] * run + a_recv[q].astype(F32)
         run_d = run_d * dec_e[q : q + 1, :]
 
-    onward = remote(t_send, b_recv, b_s, b_r, {"seq": lax.rem(me + seg_len, n_seq)})
-
-    @pl.when(seg > 0)
-    def _():
-        onward.wait_recv()
-
-    carry = b_recv[0]
-    t_send[...] = (run + run_d * carry)[None]
+    seg_ld = ld_recv[0]
+    for q in range(1, seg_len):
+        seg_ld = seg_ld + ld_recv[q]
+    after = {"seq": lax.rem(me + seg_len, n_seq)}
+    onward = [
+        remote(t_send, b_recv, b_s, b_r, after),
+        remote(lx_mine, lx_recv, bl_s, bl_r, after),
+    ]
+    sends = (seg >= 1) & (seg + 1 < segs)
+
+    @pl.when(seg >= 2)
+    def _():
+        for copy in onward:
+            copy.wait_recv()
+
+    t_send[...] = (run + run_d * b_recv[0])[None]
+    lx_mine[...] = lx_recv[...] + seg_ld[None]
 
     @pl.when(seg + 1 < segs)
     def _():
         pl.semaphore_wait(ready_b, 1)
-        onward.start()
-
+
+    @pl.when(sends)
+    def _():
+        for copy in onward:
+            copy.start()
+
+    first_up = remote(f_recv, f_recv, f_s, f_r, after)
+    first_down = remote(f_recv, f_recv, f_s, f_r, {"seq": lax.rem(me + n_seq - seg_len, n_seq)})
+    first_wrap = remote(f_recv, f_recv, fw_s, f_r, {"seq": lax.rem(me + (segs - 1) * seg_len, n_seq)})
+
+    @pl.when(seg == 0)
+    def _():
+        f_recv[...] = run[None]
+
+    @pl.when(seg >= 1)
+    def _():
+        first_up.wait_recv()
+
+    @pl.when(seg < middle)
+    def _():
+        first_up.start()
+
+    @pl.when(seg >= middle + 2)
+    def _():
+        first_down.start()
+
+    carry = b_recv[0] + jnp.exp2(widen3(jnp.broadcast_to(lx_recv[0], (8, LANES))))[0:1, :] * f_recv[0]
+    carry = jnp.where(seg == 0, jnp.zeros_like(carry), carry)
     for q in range(seg_len):
         c_send[q] = loc[q] + before[q] * carry
 
@@ -370,6 +410,13 @@
             copy.start()
 
     inc[pl.ds(pos, 1)] = c_send[pl.ds(pos, 1)]
+    if wrap:
+
+        @pl.when(seg == 0)
+        def _():
+            pl.semaphore_wait(ready_w, 1)
+            first_wrap.start()
+
     lax.fori_loop(0, jnp.where(me == 0, groups, 0), inside, 0)
 
     @pl.when(me > 0)
@@ -387,10 +434,12 @@
         state = entry[g] + run_d * inc[...].reshape(STATE, feat)
         high, low = two_parts(state)
         c_rows = bconv[r0 : r0 + GROUP, STATE:]
+        c_rows = jnp.concatenate([c_rows, c_rows], axis=1)
+        both = jnp.concatenate([high, low], axis=0)
         squares = jnp.zeros((GROUP, LANES), F32)
         for j in range(tiles):
             c0 = j * LANES
-            carried = dot(c_rows, high[:, c0 : c0 + LANES]) + dot(c_rows, low[:, c0 : c0 + LANES])
+            carried = dot(c_rows, both[:, c0 : c0 + LANES])
             gated = base[r0 : r0 + GROUP, c0 : c0 + LANES] + scale[r0 : r0 + GROUP, c0 : c0 + LANES] * carried
             base[r0 : r0 + GROUP, c0 : c0 + LANES] = gated
             squares = squares + gated * gated
@@ -431,9 +480,24 @@
         for copy in halos:
             copy.wait_send()
 
-    @pl.when(seg + 1 < segs)
-    def _():
-        onward.wait_send()
+    @pl.when(sends)
+    def _():
+        for copy in onward:
+            copy.wait_send()
+
+    @pl.when(seg < middle)
+    def _():
+        first_up.wait_send()
+
+    @pl.when(seg >= middle + 2)
+    def _():
+        first_down.wait_send()
+
+    if wrap:
+
+        @pl.when(seg == 0)
+        def _():
+            first_wrap.wait_send()
 
     for wanted, copy in c_copies:
 
@@ -467,14 +531,15 @@
         pltpu.VMEM((length, feat), BF16),
         pltpu.VMEM((length, feat), BF16),
         pltpu.VMEM((length, 2 * STATE), BF16),
-        pltpu.VMEM((LANES, length), F32),
+        pltpu.VMEM((16, length), F32),
+        pltpu.VMEM((feat // LANES + 2, ROWS + HALO, LANES), F32),
         pltpu.VMEM((length, LANES), F32),
         pltpu.VMEM((length, LANES), F32),
         pltpu.VMEM((groups, 16, GROUP), F32),
         pltpu.VMEM((groups, 16, GROUP), F32),
         pltpu.VMEM((8, LANES), F32),
         pltpu.VMEM((8, feat + 2 * STATE), F32),
-        pltpu.VMEM((LANES, feat), BF16),
+        pltpu.VMEM((2 * LANES, feat), BF16),
         pltpu.VMEM((GROUP, GROUP), BF16),
         pltpu.VMEM((GROUP, feat), F32),
         pltpu.VMEM((GROUP, feat), BF16),
@@ -489,16 +554,19 @@
         pltpu.VMEM((seg_len, piece, feat), F32),
         pltpu.VMEM((1, piece, feat), F32),
         pltpu.VMEM((1, piece, feat), F32),
+        pltpu.VMEM((1, 1, LANES), F32),
+        pltpu.VMEM((1, 1, LANES), F32),
+        pltpu.VMEM((1, piece, feat), F32),
         pltpu.VMEM((seg_len, piece, feat), F32),
         pltpu.VMEM((seg_len, piece, feat), F32),
         pltpu.VMEM((1, 8, LANES), F32),
         pltpu.VMEM((n_head, 8, LANES), F32),
-        regular, regular((seg_len,)), regular,
+        regular, regular((seg_len,)), regular, regular,
         dma((11,)),
         dma((2,)), dma((2,)),
         dma((seg_len,)), dma((seg_len,)),
         dma((seg_len,)), dma((seg_len,)),
-        dma, dma,
+        dma, dma, dma, dma, dma, dma, dma,
         dma((seg_len,)), dma((seg_len,)),
         dma((n_head,)), dma((n_head,)),
     ]

time: 71.7 us -> 83.5 us (1.16)
  the two profiles are of different devices: /device:TPU:1826 before, /device:TPU:1314 now
where the time goes in v4:
time: 83.5 us; the launch traced here: 83.4 us
  Pallas kernels  82.1 us (98%)
  other arithmetic  1.25 us (1%)
    pallas_call x1, Pallas kernels, on_device(): pl.pallas_call(functools.partial(kernel, sizes), out_shape=jax.ShapeDtype...  82.1 us

profile of v4, /device:TPU:1314, one launch (start us, length us, event | category | flops | bytes accessed | tf_op | source)
XLA Modules:
  0.0 83.4 jit_solution(16233473378178757290)
XLA Ops:
  0.0 0.0 copy-start
  0.0 82.1 %ssd_layer.1 = f32[1024,640]{1,0:T(8,128)S(1)} custom-call(bf16[1024,640]{1,0:T(8,128)(2,1)} %bitcast.9, bf16[1024,256]{1,0:T(8,128)(2,1)} %bitcast.11, bf16[1024,640]{1,0:T(8,128)(2,1)} %bitcast.10, f32[10,1,1024]{2,1,0:T(1,128)} %bitcast.12, bf16[4,640]{1,0:T(4,128)(2,1)} %refs_4_.1, bf16[640]{0:T(1024)(128)(2,1)} %refs_5_.1, bf16[4,256]{1,0:T(4,128)(2,1)} %refs_6_.1, ...), custom_call_target="tpu_custom_call" | custom-call | tf_op jit(solution)/shard_map/ssd_layer/pallas_call | solution.py:575
  82.1 0.0 copy-done
  82.1 1.2 %fusion = bf16[1,1024,640]{2,1,0:T(8,128)(2,1)} fusion(f32[1024,640]{1,0:T(8,128)S(1)} %ssd_layer.1, f32[640]{0:T(1024)S(1)} %copy-done), kind=kLoop, calls=%fused_computation.1 | loop fusion | flops 1310720 | bytes 3934720 | tf_op jit(solution)/shard_map/broadcast_in_dim | solution.py:591
Async XLA Ops:
  0.0 82.1 %copy-start = (f32[640]{0:T(1024)S(1)}, f32[640]{0:T(1024)}, u32[]{:S(2)}) copy-start(f32[640]{0:T(1024)} %param.23) | copy-start | bytes 7684

commit v5 on v4

--- a/solution.py
+++ b/solution.py
@@ -15,6 +15,7 @@
 HALO = 16
 ROWS = 64
 SEG = 4
+SUB = 4
 VMEM_LIMIT = 30 * 1024 * 1024
 LOG2E = 1.4426950408889634
 norm_eps = 1e-05
@@ -52,9 +53,9 @@
         step_ref, cxw_ref, cxb_ref, cbw_ref, cbb_ref, dt_ref, alog_ref, skip_ref,
         xext, bcext, gbuf, xconv, bconv, raw_t, shifts, stepb, ldb, ldt, stept, par, cw, expand_m, tri_m,
         tail_e, weighted, fresh, entry, scale, dec,
-        s_send, a_recv, ld_mine, ld_recv, loc, t_send, b_recv, lx_mine, lx_recv, f_recv, c_send, inc,
-        ss_mine, ss_recv, ready_h, ready_a, ready_b, ready_w,
-        loc_sem, halo_s, halo_r, a_s, a_r, al_s, al_r, b_s, b_r, bl_s, bl_r, f_s, f_r, fw_s, c_s, c_r, x_s, x_r,
+        s_send, a_recv, ld_mine, ld_recv, loc, t_send, b_recv, c_send, inc,
+        ss_mine, ss_recv, ready_h, ready_a, ready_b,
+        loc_sem, halo_s, halo_r, a_s, a_r, al_s, al_r, b_s, b_r, c_s, c_r, x_s, x_r,
     ) = refs
     groups = length // GROUP
     tiles = feat // LANES
@@ -62,13 +63,10 @@
     segs = n_seq // seg_len
     di = feat * n_head
 
-    middle = segs // 2
-    wrap = segs - 1 > middle
     me = lax.axis_index("seq")
     mine_h = lax.axis_index("head")
     seg = me // seg_len
     pos = lax.rem(me, seg_len)
-    last_seg = jnp.where(seg == segs - 1, 1, 0) if wrap else 0
 
     loads = [
         pltpu.make_async_copy(x_hbm, xext.at[pl.ds(HALO, length)], loc_sem.at[0]),
@@ -87,7 +85,6 @@
         load.start()
 
     b_recv[...] = jnp.zeros_like(b_recv)
-    lx_recv[...] = jnp.zeros_like(lx_recv)
     inc[...] = jnp.zeros_like(inc)
     barrier = pltpu.get_barrier_semaphore()
 
@@ -107,12 +104,6 @@
     @pl.when(seg + 1 < segs)
     def _():
         greet({"seq": me + seg_len})
-
-    if wrap:
-
-        @pl.when(seg == 0)
-        def _():
-            greet({"seq": me + (segs - 1) * seg_len})
 
     for d in range(1, n_head):
         greet({"head": lax.rem(mine_h + d, n_head)})
@@ -186,7 +177,7 @@
         tail_e[...] = widen2(tail)
 
         def chunk(i, inner):
-            q0 = pl.multiple_of(i * ROWS, ROWS)
+            q0 = i * ROWS
             r = pl.multiple_of(r0 + q0, ROWS)
             for j in range(2 * STATE // LANES):
                 bconv[pl.ds(r, ROWS), j * LANES : (j + 1) * LANES] = conv(bcext, r, j, feat).astype(BF16)
@@ -199,7 +190,8 @@
                 ).astype(BF16)
             return inner
 
-        lax.fori_loop(0, GROUP // ROWS, chunk, 0)
+        for i in range(GROUP // ROWS):
+            chunk(i, 0)
         fresh[pl.ds(g, 1)] = dot(
             bconv[pl.ds(r0, GROUP), 0:STATE], weighted[...], ((0,), (0,))
         )[None]
@@ -211,7 +203,7 @@
 
     @pl.when(me > 0)
     def _():
-        pl.semaphore_wait(barrier, 1 + pos + jnp.where(seg > 0, 1, 0) + n_head - 1 + last_seg)
+        pl.semaphore_wait(barrier, 1 + pos + jnp.where(seg > 0, 1, 0) + n_head - 1)
         pl.semaphore_signal(ready_h, inc=1, device_id={"seq": me - 1}, device_id_type=MESH)
 
     for d in range(1, seg_len):
@@ -223,12 +215,6 @@
     @pl.when(seg > 0)
     def _():
         pl.semaphore_signal(ready_b, inc=1, device_id={"seq": me - seg_len}, device_id_type=MESH)
-
-    if wrap:
-
-        @pl.when(seg == segs - 1)
-        def _():
-            pl.semaphore_signal(ready_w, inc=1, device_id={"seq": me - (segs - 1) * seg_len}, device_id_type=MESH)
 
     def remote(src, dst, send, recv, where):
         return pltpu.make_async_remote_copy(
@@ -346,55 +332,30 @@
         run = dec_e[q : q + 1, :] * run + a_recv[q].astype(F32)
         run_d = run_d * dec_e[q : q + 1, :]
 
-    seg_ld = ld_recv[0]
-    for q in range(1, seg_len):
-        seg_ld = seg_ld + ld_recv[q]
     after = {"seq": lax.rem(me + seg_len, n_seq)}
+    rows = piece // SUB
     onward = [
-        remote(t_send, b_recv, b_s, b_r, after),
-        remote(lx_mine, lx_recv, bl_s, bl_r, after),
+        remote(t_send.at[pl.ds(u, 1)], b_recv.at[pl.ds(u, 1)], b_s.at[u], b_r.at[u], after)
+        for u in range(SUB)
     ]
-    sends = (seg >= 1) & (seg + 1 < segs)
-
-    @pl.when(seg >= 2)
-    def _():
-        for copy in onward:
-            copy.wait_recv()
-
-    t_send[...] = (run + run_d * b_recv[0])[None]
-    lx_mine[...] = lx_recv[...] + seg_ld[None]
 
     @pl.when(seg + 1 < segs)
     def _():
         pl.semaphore_wait(ready_b, 1)
 
-    @pl.when(sends)
-    def _():
-        for copy in onward:
-            copy.start()
-
-    first_up = remote(f_recv, f_recv, f_s, f_r, after)
-    first_down = remote(f_recv, f_recv, f_s, f_r, {"seq": lax.rem(me + n_seq - seg_len, n_seq)})
-    first_wrap = remote(f_recv, f_recv, fw_s, f_r, {"seq": lax.rem(me + (segs - 1) * seg_len, n_seq)})
-
-    @pl.when(seg == 0)
-    def _():
-        f_recv[...] = run[None]
-
-    @pl.when(seg >= 1)
-    def _():
-        first_up.wait_recv()
-
-    @pl.when(seg < middle)
-    def _():
-        first_up.start()
-
-    @pl.when(seg >= middle + 2)
-    def _():
-        first_down.start()
-
-    carry = b_recv[0] + jnp.exp2(widen3(jnp.broadcast_to(lx_recv[0], (8, LANES))))[0:1, :] * f_recv[0]
-    carry = jnp.where(seg == 0, jnp.zeros_like(carry), carry)
+    for u in range(SUB):
+
+        @pl.when(seg > 0)
+        def _():
+            onward[u].wait_recv()
+
+        t_send[u] = run[u * rows : (u + 1) * rows] + run_d * b_recv[u]
+
+        @pl.when(seg + 1 < segs)
+        def _():
+            onward[u].start()
+
+    carry = b_recv[...].reshape(piece, feat)
     for q in range(seg_len):
         c_send[q] = loc[q] + before[q] * carry
 
@@ -410,13 +371,6 @@
             copy.start()
 
     inc[pl.ds(pos, 1)] = c_send[pl.ds(pos, 1)]
-    if wrap:
-
-        @pl.when(seg == 0)
-        def _():
-            pl.semaphore_wait(ready_w, 1)
-            first_wrap.start()
-
     lax.fori_loop(0, jnp.where(me == 0, groups, 0), inside, 0)
 
     @pl.when(me > 0)
@@ -480,24 +434,10 @@
         for copy in halos:
             copy.wait_send()
 
-    @pl.when(sends)
+    @pl.when(seg + 1 < segs)
     def _():
         for copy in onward:
             copy.wait_send()
-
-    @pl.when(seg < middle)
-    def _():
-        first_up.wait_send()
-
-    @pl.when(seg >= middle + 2)
-    def _():
-        first_down.wait_send()
-
-    if wrap:
-
-        @pl.when(seg == 0)
-        def _():
-            first_wrap.wait_send()
 
     for wanted, copy in c_copies:
 
@@ -552,21 +492,18 @@
         pltpu.VMEM((1, 1, LANES), F32),
         pltpu.VMEM((seg_len, 1, LANES), F32),
         pltpu.VMEM((seg_len, piece, feat), F32),
-        pltpu.VMEM((1, piece, feat), F32),
-        pltpu.VMEM((1, piece, feat), F32),
-        pltpu.VMEM((1, 1, LANES), F32),
-        pltpu.VMEM((1, 1, LANES), F32),
-        pltpu.VMEM((1, piece, feat), F32),
+        pltpu.VMEM((SUB, piece // SUB, feat), F32),
+        pltpu.VMEM((SUB, piece // SUB, feat), F32),
         pltpu.VMEM((seg_len, piece, feat), F32),
         pltpu.VMEM((seg_len, piece, feat), F32),
         pltpu.VMEM((1, 8, LANES), F32),
         pltpu.VMEM((n_head, 8, LANES), F32),
-        regular, regular((seg_len,)), regular, regular,
+        regular, regular((seg_len,)), regular,
         dma((11,)),
         dma((2,)), dma((2,)),
         dma((seg_len,)), dma((seg_len,)),
         dma((seg_len,)), dma((seg_len,)),
-        dma, dma, dma, dma, dma, dma, dma,
+        dma((SUB,)), dma((SUB,)),
         dma((seg_len,)), dma((seg_len,)),
         dma((n_head,)), dma((n_head,)),
     ]

time: 83.5 us -> 63.7 us (0.76)
  the two profiles are of different devices: /device:TPU:1314 before, /device:TPU:290 now
where the time goes in v5:
time: 63.7 us; the launch traced here: 63.6 us
  Pallas kernels  62.3 us (98%)
  other arithmetic  1.25 us (2%)
    pallas_call x1, Pallas kernels, on_device(): pl.pallas_call(functools.partial(kernel, sizes), out_shape=jax.ShapeDtype...  62.3 us

profile of v5, /device:TPU:290, one launch (start us, length us, event | category | flops | bytes accessed | tf_op | source)
XLA Modules:
  0.0 63.6 jit_solution(5475248727187644610)
XLA Ops:
  0.0 0.0 copy-start
  0.0 62.3 %ssd_layer.1 = f32[1024,640]{1,0:T(8,128)S(1)} custom-call(bf16[1024,640]{1,0:T(8,128)(2,1)} %bitcast.9, bf16[1024,256]{1,0:T(8,128)(2,1)} %bitcast.11, bf16[1024,640]{1,0:T(8,128)(2,1)} %bitcast.10, f32[10,1,1024]{2,1,0:T(1,128)} %bitcast.12, bf16[4,640]{1,0:T(4,128)(2,1)} %refs_4_.1, bf16[640]{0:T(1024)(128)(2,1)} %refs_5_.1, bf16[4,256]{1,0:T(4,128)(2,1)} %refs_6_.1, ...), custom_call_target="tpu_custom_call" | custom-call | tf_op jit(solution)/shard_map/ssd_layer/pallas_call | solution.py:512
  62.4 0.0 copy-done
  62.4 1.2 %fusion = bf16[1,1024,640]{2,1,0:T(8,128)(2,1)} fusion(f32[1024,640]{1,0:T(8,128)S(1)} %ssd_layer.1, f32[640]{0:T(1024)S(1)} %copy-done), kind=kLoop, calls=%fused_computation.1 | loop fusion | flops 1310720 | bytes 3934720 | tf_op jit(solution)/shard_map/broadcast_in_dim | solution.py:528
Async XLA Ops:
  0.0 62.4 %copy-start = (f32[640]{0:T(1024)S(1)}, f32[640]{0:T(1024)}, u32[]{:S(2)}) copy-start(f32[640]{0:T(1024)} %param.23) | copy-start | bytes 7684

commit v6 on v5

--- a/solution.py
+++ b/solution.py
@@ -52,7 +52,7 @@
         dt_hbm, alog_hbm, skip_hbm, base,
         step_ref, cxw_ref, cxb_ref, cbw_ref, cbb_ref, dt_ref, alog_ref, skip_ref,
         xext, bcext, gbuf, xconv, bconv, raw_t, shifts, stepb, ldb, ldt, stept, par, cw, expand_m, tri_m,
-        tail_e, weighted, fresh, entry, scale, dec,
+        tail_e, weighted, fresh, entry, scale, dec, gdec,
         s_send, a_recv, ld_mine, ld_recv, loc, t_send, b_recv, c_send, inc,
         ss_mine, ss_recv, ready_h, ready_a, ready_b,
         loc_sem, halo_s, halo_r, a_s, a_r, al_s, al_r, b_s, b_r, c_s, c_r, x_s, x_r,
@@ -199,8 +199,6 @@
 
     for load in loads[:2]:
         load.wait()
-    lax.fori_loop(1, groups, states, 0)
-
     @pl.when(me > 0)
     def _():
         pl.semaphore_wait(barrier, 1 + pos + jnp.where(seg > 0, 1, 0) + n_head - 1)
@@ -227,11 +225,24 @@
         remote(bcext.at[pl.ds(length, HALO)], bcext.at[pl.ds(0, HALO)], halo_s.at[1], halo_r.at[1], {"seq": lax.rem(me + 1, n_seq)}),
     ]
 
-    @pl.when(me + 1 < n_seq)
-    def _():
-        pl.semaphore_wait(ready_h, 1)
-        for copy in halos:
-            copy.start()
+    def states_and_halo(g, carry):
+        @pl.when((g == min(2, groups - 1)) & (me + 1 < n_seq))
+        def _():
+            pl.semaphore_wait(ready_h, 1)
+            for copy in halos:
+                copy.start()
+
+        return states(g, carry)
+
+    lax.fori_loop(1, groups, states_and_halo, 0)
+
+    def far_first(copies, wanted):
+        for m in range(seg_len - 1, 0, -1):
+            for inside_seg, to, d in ((pos + m < seg_len, pos + m, m), (pos >= m, pos - m, seg_len - m)):
+
+                @pl.when(inside_seg & wanted(to))
+                def _():
+                    copies[d - 1].start()
 
     def seg_peer(d):
         return {"seq": seg * seg_len + lax.rem(pos + d, seg_len)}
@@ -279,8 +290,7 @@
         a_copies.append(
             remote(s_send.at[pl.ds(to, 1)], a_recv.at[pl.ds(pos, 1)], a_s.at[d - 1], a_r.at[d - 1], seg_peer(d))
         )
-    for copy in reversed(a_copies):
-        copy.start()
+    far_first(a_copies, lambda to: True)
     a_recv[pl.ds(pos, 1)] = s_send[pl.ds(pos, 1)]
 
     skip_e = widen3(par[...])[2:3, :]
@@ -315,7 +325,35 @@
         return carry
 
     loads[2].wait()
-    lax.fori_loop(0, jnp.where(me == 0, 0, groups), inside, 0)
+    lax.fori_loop(0, groups, inside, 0)
+
+    blocks = GROUP // 8
+    lane8 = lax.broadcasted_iota(jnp.int32, (blocks, 8, LANES), 2)
+    block_i = lax.broadcasted_iota(jnp.int32, (blocks, 8, LANES), 0)
+    gdec[0:groups, :] = group_decay[0:groups, :]
+
+    def finish(g, so_far):
+        run_d, ss = so_far
+        r0 = pl.multiple_of(g * GROUP, GROUP)
+        state = entry[g] + run_d * inc[...].reshape(STATE, feat)
+        high, low = two_parts(state)
+        c_rows = bconv[pl.ds(r0, GROUP), STATE:]
+        c_rows = jnp.concatenate([c_rows, c_rows], axis=1)
+        both = jnp.concatenate([high, low], axis=0)
+        squares = jnp.zeros((GROUP, LANES), F32)
+        for j in range(tiles):
+            c0 = j * LANES
+            carried = dot(c_rows, both[:, c0 : c0 + LANES])
+            gated = base[pl.ds(r0, GROUP), c0 : c0 + LANES] + scale[pl.ds(r0, GROUP), c0 : c0 + LANES] * carried
+            base[pl.ds(r0, GROUP), c0 : c0 + LANES] = gated
+            squares = squares + gated * gated
+        total = jnp.broadcast_to(jnp.sum(squares, axis=1, keepdims=True), (GROUP, LANES))
+        total = total.reshape(blocks, 8, LANES)
+        ss = ss + jnp.sum(jnp.where(lane8 == block_i + g * blocks, total, 0.0), axis=0)
+        return run_d * gdec[pl.ds(g, 1), :], ss
+
+    nothing = (jnp.ones((1, feat), F32), jnp.zeros((8, LANES), F32))
+    _, ss_early = lax.fori_loop(0, jnp.where(me == 0, groups, 0), finish, nothing)
 
     for copy in ld_copies:
         copy.wait()
@@ -364,43 +402,16 @@
         to = lax.rem(pos + d, seg_len)
         copy = remote(c_send.at[pl.ds(to, 1)], inc.at[pl.ds(pos, 1)], c_s.at[d - 1], c_r.at[d - 1], seg_peer(d))
         c_copies.append((seg + to > 0, copy))
-    for wanted, copy in c_copies:
-
-        @pl.when(wanted)
-        def _():
-            copy.start()
-
+    far_first([copy for _, copy in c_copies], lambda to: seg + to > 0)
     inc[pl.ds(pos, 1)] = c_send[pl.ds(pos, 1)]
-    lax.fori_loop(0, jnp.where(me == 0, groups, 0), inside, 0)
 
     @pl.when(me > 0)
     def _():
         for _, copy in c_copies:
             copy.wait_recv()
 
-    run_d = jnp.ones((1, feat), F32)
-    ss = jnp.zeros((8, LANES), F32)
-    blocks = GROUP // 8
-    lane8 = lax.broadcasted_iota(jnp.int32, (blocks, 8, LANES), 2)
-    block_i = lax.broadcasted_iota(jnp.int32, (blocks, 8, LANES), 0)
-    for g in range(groups):
-        r0 = g * GROUP
-        state = entry[g] + run_d * inc[...].reshape(STATE, feat)
-        high, low = two_parts(state)
-        c_rows = bconv[r0 : r0 + GROUP, STATE:]
-        c_rows = jnp.concatenate([c_rows, c_rows], axis=1)
-        both = jnp.concatenate([high, low], axis=0)
-        squares = jnp.zeros((GROUP, LANES), F32)
-        for j in range(tiles):
-            c0 = j * LANES
-            carried = dot(c_rows, both[:, c0 : c0 + LANES])
-            gated = base[r0 : r0 + GROUP, c0 : c0 + LANES] + scale[r0 : r0 + GROUP, c0 : c0 + LANES] * carried
-            base[r0 : r0 + GROUP, c0 : c0 + LANES] = gated
-            squares = squares + gated * gated
-        total = jnp.broadcast_to(jnp.sum(squares, axis=1, keepdims=True), (GROUP, LANES))
-        total = total.reshape(blocks, 8, LANES)
-        ss = ss + jnp.sum(jnp.where(lane8 == block_i + g * blocks, total, 0.0), axis=0)
-        run_d = run_d * group_decay[g : g + 1, :]
+    _, ss_late = lax.fori_loop(0, jnp.where(me == 0, 0, groups), finish, nothing)
+    ss = ss_early + ss_late
     ss_mine[...] = ss[None]
 
     @pl.when(me == 0)
@@ -487,6 +498,7 @@
         pltpu.VMEM((groups, STATE, feat), F32),
         pltpu.VMEM((length, feat), F32),
         pltpu.VMEM((8, LANES), F32),
+        pltpu.VMEM((8, feat), F32),
         pltpu.VMEM((seg_len, piece, feat), BF16),
         pltpu.VMEM((seg_len, piece, feat), BF16),
         pltpu.VMEM((1, 1, LANES), F32),

time: 63.7 us -> 65.6 us (1.030)
  Pallas kernels: 62.3 us -> 64.2 us
    pallas_call x1, Pallas kernels: 62.3 us -> 64.2 us  [on_device(): pl.pallas_call(functools.partial(kernel, sizes), out_shape=jax.ShapeDtype...]
where the time goes in v6:
time: 65.6 us; the launch traced here: 65.5 us
  Pallas kernels  64.2 us (98%)
  other arithmetic  1.25 us (2%)
    pallas_call x1, Pallas kernels, on_device(): pl.pallas_call(functools.partial(kernel, sizes), out_shape=jax.ShapeDtype...  64.2 us

profile of v6, /device:TPU:290, one launch (start us, length us, event | category | flops | bytes accessed | tf_op | source)
XLA Modules:
  0.0 65.5 jit_solution(16429632723803467221)
XLA Ops:
  0.0 0.0 copy-start
  0.0 64.2 %ssd_layer.1 = f32[1024,640]{1,0:T(8,128)S(1)} custom-call(bf16[1024,640]{1,0:T(8,128)(2,1)} %bitcast.9, bf16[1024,256]{1,0:T(8,128)(2,1)} %bitcast.11, bf16[1024,640]{1,0:T(8,128)(2,1)} %bitcast.10, f32[10,1,1024]{2,1,0:T(1,128)} %bitcast.12, bf16[4,640]{1,0:T(4,128)(2,1)} %refs_4_.1, bf16[640]{0:T(1024)(128)(2,1)} %refs_5_.1, bf16[4,256]{1,0:T(4,128)(2,1)} %refs_6_.1, ...), custom_call_target="tpu_custom_call" | custom-call | tf_op jit(solution)/shard_map/ssd_layer/pallas_call | solution.py:524
  64.2 0.0 copy-done
  64.2 1.2 %fusion = bf16[1,1024,640]{2,1,0:T(8,128)(2,1)} fusion(f32[1024,640]{1,0:T(8,128)S(1)} %ssd_layer.1, f32[640]{0:T(1024)S(1)} %copy-done), kind=kLoop, calls=%fused_computation.1 | loop fusion | flops 1310720 | bytes 3934720 | tf_op jit(solution)/shard_map/broadcast_in_dim | solution.py:540
Async XLA Ops:
  0.0 64.2 %copy-start = (f32[640]{0:T(1024)S(1)}, f32[640]{0:T(1024)}, u32[]{:S(2)}) copy-start(f32[640]{0:T(1024)} %param.23) | copy-start | bytes 7684

commit v7 on v6

--- a/solution.py
+++ b/solution.py
@@ -325,7 +325,8 @@
         return carry
 
     loads[2].wait()
-    lax.fori_loop(0, groups, inside, 0)
+    first_part = jnp.where(seg == 0, groups // 2, groups)
+    lax.fori_loop(0, first_part, inside, 0)
 
     blocks = GROUP // 8
     lane8 = lax.broadcasted_iota(jnp.int32, (blocks, 8, LANES), 2)
@@ -353,7 +354,6 @@
         return run_d * gdec[pl.ds(g, 1), :], ss
 
     nothing = (jnp.ones((1, feat), F32), jnp.zeros((8, LANES), F32))
-    _, ss_early = lax.fori_loop(0, jnp.where(me == 0, groups, 0), finish, nothing)
 
     for copy in ld_copies:
         copy.wait()
@@ -404,14 +404,14 @@
         c_copies.append((seg + to > 0, copy))
     far_first([copy for _, copy in c_copies], lambda to: seg + to > 0)
     inc[pl.ds(pos, 1)] = c_send[pl.ds(pos, 1)]
+    lax.fori_loop(first_part, groups, inside, 0)
 
     @pl.when(me > 0)
     def _():
         for _, copy in c_copies:
             copy.wait_recv()
 
-    _, ss_late = lax.fori_loop(0, jnp.where(me == 0, 0, groups), finish, nothing)
-    ss = ss_early + ss_late
+    _, ss = lax.fori_loop(0, groups, finish, nothing)
     ss_mine[...] = ss[None]
 
     @pl.when(me == 0)

time: 65.6 us -> 63.4 us (0.966)
  Pallas kernels: 64.2 us -> 62 us
    pallas_call x1, Pallas kernels: 64.2 us -> 62 us  [on_device(): pl.pallas_call(functools.partial(kernel, sizes), out_shape=jax.ShapeDtype...]
where the time goes in v7:
time: 63.4 us; the launch traced here: 63.2 us
  Pallas kernels  62 us (98%)
  other arithmetic  1.25 us (2%)
    pallas_call x1, Pallas kernels, on_device(): pl.pallas_call(functools.partial(kernel, sizes), out_shape=jax.ShapeDtype...  62 us

profile of v7, /device:TPU:290, one launch (start us, length us, event | category | flops | bytes accessed | tf_op | source)
XLA Modules:
  0.0 63.2 jit_solution(4373885530663080725)
XLA Ops:
  0.0 0.0 copy-start
  0.0 62.0 %ssd_layer.1 = f32[1024,640]{1,0:T(8,128)S(1)} custom-call(bf16[1024,640]{1,0:T(8,128)(2,1)} %bitcast.9, bf16[1024,256]{1,0:T(8,128)(2,1)} %bitcast.11, bf16[1024,640]{1,0:T(8,128)(2,1)} %bitcast.10, f32[10,1,1024]{2,1,0:T(1,128)} %bitcast.12, bf16[4,640]{1,0:T(4,128)(2,1)} %refs_4_.1, bf16[640]{0:T(1024)(128)(2,1)} %refs_5_.1, bf16[4,256]{1,0:T(4,128)(2,1)} %refs_6_.1, ...), custom_call_target="tpu_custom_call" | custom-call | tf_op jit(solution)/shard_map/ssd_layer/pallas_call | solution.py:524
  62.0 0.0 copy-done
  62.0 1.2 %fusion = bf16[1,1024,640]{2,1,0:T(8,128)(2,1)} fusion(f32[1024,640]{1,0:T(8,128)S(1)} %ssd_layer.1, f32[640]{0:T(1024)S(1)} %copy-done), kind=kLoop, calls=%fused_computation.1 | loop fusion | flops 1310720 | bytes 3934720 | tf_op jit(solution)/shard_map/broadcast_in_dim | solution.py:540
Async XLA Ops:
  0.0 62.0 %copy-start = (f32[640]{0:T(1024)S(1)}, f32[640]{0:T(1024)}, u32[]{:S(2)}) copy-start(f32[640]{0:T(1024)} %param.23) | copy-start | bytes 7684

commit v8 on v7

--- a/solution.py
+++ b/solution.py
@@ -325,7 +325,7 @@
         return carry
 
     loads[2].wait()
-    first_part = jnp.where(seg == 0, groups // 2, groups)
+    first_part = jnp.where(seg == 0, groups // 4, groups)
     lax.fori_loop(0, first_part, inside, 0)
 
     blocks = GROUP // 8

time: 63.4 us -> 63.4 us (level)
  no operation moved by 1% of the time
where the time goes in v8:
time: 63.4 us; the launch traced here: 63.2 us
  Pallas kernels  62 us (98%)
  other arithmetic  1.25 us (2%)
    pallas_call x1, Pallas kernels, on_device(): pl.pallas_call(functools.partial(kernel, sizes), out_shape=jax.ShapeDtype...  62 us

profile of v8, /device:TPU:290, one launch (start us, length us, event | category | flops | bytes accessed | tf_op | source)
XLA Modules:
  0.0 63.2 jit_solution(12790895930820888323)
XLA Ops:
  0.0 0.0 copy-start
  0.0 62.0 %ssd_layer.1 = f32[1024,640]{1,0:T(8,128)S(1)} custom-call(bf16[1024,640]{1,0:T(8,128)(2,1)} %bitcast.9, bf16[1024,256]{1,0:T(8,128)(2,1)} %bitcast.11, bf16[1024,640]{1,0:T(8,128)(2,1)} %bitcast.10, f32[10,1,1024]{2,1,0:T(1,128)} %bitcast.12, bf16[4,640]{1,0:T(4,128)(2,1)} %refs_4_.1, bf16[640]{0:T(1024)(128)(2,1)} %refs_5_.1, bf16[4,256]{1,0:T(4,128)(2,1)} %refs_6_.1, ...), custom_call_target="tpu_custom_call" | custom-call | tf_op jit(solution)/shard_map/ssd_layer/pallas_call | solution.py:524
  62.0 0.0 copy-done
  62.0 1.2 %fusion = bf16[1,1024,640]{2,1,0:T(8,128)(2,1)} fusion(f32[1024,640]{1,0:T(8,128)S(1)} %ssd_layer.1, f32[640]{0:T(1024)S(1)} %copy-done), kind=kLoop, calls=%fused_computation.1 | loop fusion | flops 1310720 | bytes 3934720 | tf_op jit(solution)/shard_map/broadcast_in_dim | solution.py:540
Async XLA Ops:
  0.0 62.0 %copy-start = (f32[640]{0:T(1024)S(1)}, f32[640]{0:T(1024)}, u32[]{:S(2)}) copy-start(f32[640]{0:T(1024)} %param.23) | copy-start | bytes 7684
